TPU v7x, 32 devices: a whole 2x2x4 slice. The times are simulated.
32 devices in a mesh: ctx: 8 (over y, x, core), tp: 4 (over z).
Axes of the slice: x: 2, y: 2, z: 4, core: 2. Of those that a mesh axis runs over, the one named last changes fastest.
Arguments:
- tokens: bfloat16 [4096, 4096], P('ctx'), may hold values from -48 to 48
- w_query: bfloat16 [4096, 4096], P(None, 'tp'), may hold values from -0.09375 to 0.09375
- w_key: bfloat16 [4096, 4096], P(None, 'tp'), may hold values from -0.09375 to 0.09375
- w_value: bfloat16 [4096, 4096], P(None, 'tp'), may hold values from -0.09375 to 0.09375
- w_out: bfloat16 [4096, 4096], P('tp'), may hold values from -0.09375 to 0.09375
- block_doc: int32 [64], replicated, may hold values from 0 to 1, never falling along the last dimension, each value on 1 to 56 neighbouring positions
- grad_out: bfloat16 [4096, 4096], P('ctx', 'tp'), may hold values from -6 to 6
Outputs:
- output: bfloat16 [4096, 4096], P('ctx', 'tp')
- grad_tokens: bfloat16 [4096, 4096], P('ctx', 'tp')
- grad_query_weight: float32 [4096, 4096], P('ctx', 'tp')
- grad_key_weight: float32 [4096, 4096], P('ctx', 'tp')
- grad_value_weight: float32 [4096, 4096], P('ctx', 'tp')
- grad_out_weight: float32 [4096, 4096], P('tp', 'ctx')
Inputs may be any that keep to these rules, and one draw needn't show every extreme that they name: block_doc never falls along the blocks; each document covers 1 to 56 consecutive blocks.
All inputs are finite; a program needn't handle non-finite values.
Results may differ from a plain program's by a relative error of at most 0.024.
The roundings to bfloat16 on the way count: a program that leaves them out, or rounds other values in their place, can miss the bound.
Values may be sent and summed in bfloat16 or wider, within the bound.
A program may use at most 192 MiB of HBM per device.

v0:
```python
import math

import jax
import jax.numpy as jnp
from jax import lax
from jax.sharding import PartitionSpec as P

HDIM = 128
BLOCK = 64


big_negative = -1e30


def elementwise_product(pattern, left_side, right_side):
    return jnp.einsum(pattern, left_side, right_side, preferred_element_type=jnp.float32)


def attend(
    query_row_matrix,
    key_row_matrix,
    value_row_matrix,
    summary_key,
    summary_value,
    allowed,
    causal,
    score_scale_factor,
):
    near_scores = (
        elementwise_product("nqhd,nkhd->nhqk", query_row_matrix, key_row_matrix)
        * score_scale_factor
    )
    near_scores = jnp.where(causal[None, None], near_scores, big_negative)
    distant_score_matrix = (
        elementwise_product("yzxo,lxo->yzxl", query_row_matrix, summary_key) * score_scale_factor
    )
    distant_score_matrix = jnp.where(allowed[:, None, None, :], distant_score_matrix, big_negative)
    row_top = jnp.maximum(
        jnp.transpose(jnp.max(near_scores, axis=3), (0, 2, 1)),
        jnp.max(distant_score_matrix, axis=3),
    )
    near_exp = jnp.exp(near_scores - jnp.transpose(row_top, (0, 2, 1))[..., None])
    far_exp = jnp.exp(distant_score_matrix - row_top[..., None])
    denom_sum = jnp.transpose(jnp.sum(near_exp, axis=3), (0, 2, 1)) + jnp.sum(far_exp, axis=3)
    local_weight = (near_exp / jnp.transpose(denom_sum, (0, 2, 1))[..., None]).astype(jnp.bfloat16)
    distant_weight = (far_exp / denom_sum[..., None]).astype(jnp.bfloat16)
    combined_output = elementwise_product(
        "jvyb,jbvo->jyvo", local_weight, value_row_matrix
    ) + elementwise_product("gtuv,vuk->gtuk", distant_weight, summary_value)
    return (combined_output.astype(jnp.bfloat16), local_weight, distant_weight)


def attend_back(
    query_row_matrix,
    key_row_matrix,
    value_row_matrix,
    summary_key,
    summary_value,
    combined_output,
    local_weight,
    distant_weight,
    incoming_gradient,
    score_scale_factor,
):
    row_delta = jnp.sum(
        combined_output.astype(jnp.float32) * incoming_gradient.astype(jnp.float32), axis=3
    )
    near_d = elementwise_product("nqhd,nkhd->nhqk", incoming_gradient, value_row_matrix)
    distant_gradient_term = elementwise_product("yzxo,lxo->yzxl", incoming_gradient, summary_value)
    local_score_sum = (
        local_weight.astype(jnp.float32) * (near_d - jnp.transpose(row_delta, (0, 2, 1))[..., None])
    ).astype(jnp.bfloat16)
    distant_score_sum = (
        distant_weight.astype(jnp.float32) * (distant_gradient_term - row_delta[..., None])
    ).astype(jnp.bfloat16)
    query_gradient = (
        elementwise_product("jvyb,jbvo->jyvo", local_score_sum, key_row_matrix)
        + elementwise_product("gtuv,vuk->gtuk", distant_score_sum, summary_key)
    ) * score_scale_factor
    d_key = (
        elementwise_product("nhqk,nqhd->nkhd", local_score_sum, query_row_matrix)
        * score_scale_factor
    )
    d_value = elementwise_product("nhqk,nqhd->nkhd", local_weight, incoming_gradient)
    summary_key_gradient = (
        elementwise_product("agwi,agwu->iwu", distant_score_sum, query_row_matrix)
        * score_scale_factor
    )
    summary_value_gradient = elementwise_product(
        "agwi,agwu->iwu", distant_weight, incoming_gradient
    )
    return (query_gradient, d_key, d_value, summary_key_gradient, summary_value_gradient)


def back_project(grad_rows, weight):
    return lax.dot_general(
        grad_rows, weight, (((1,), (1,)), ((), ())), preferred_element_type=jnp.float32
    )


def term_maker(tokens, grad_rows):
    return lax.dot_general(
        tokens, grad_rows, (((0,), (0,)), ((), ())), preferred_element_type=jnp.float32
    )


def scatter_sum(partial, axis):
    count = lax.axis_size(axis)
    me = lax.axis_index(axis)
    width = partial.shape[1] // count

    def block(shift):
        return lax.dynamic_slice_in_dim(partial, ((me + shift) % count) * width, width, 1)

    total = block(0)
    for shift in range(1, count):
        ring = [(source, (source + shift) % count) for source in range(count)]
        moved = lax.ppermute(block(shift).astype(jnp.bfloat16), axis, ring)
        total = total + moved.astype(jnp.float32)
    return total


def per_device(tokens, w_query, w_key, w_value, w_out, block_doc, grad_out):
    score_scale_factor = 1.0 / math.sqrt(HDIM)
    tok_rows = tokens.shape[0]
    col_count = w_query.shape[1]
    blocks = tok_rows // BLOCK
    head_count = col_count // HDIM
    block_shape = (blocks, BLOCK, head_count, HDIM)

    def project(weight):
        return jnp.dot(tokens, weight, preferred_element_type=jnp.float32).astype(jnp.bfloat16)

    query_row_matrix = project(w_query).reshape(block_shape)
    key_row_matrix = project(w_key).reshape(block_shape)
    value_row_matrix = project(w_value).reshape(block_shape)
    own_key = key_row_matrix[:, BLOCK - 1].reshape(blocks, col_count)
    own_value = value_row_matrix[:, BLOCK - 1].reshape(blocks, col_count)
    summary = lax.all_gather(
        jnp.concatenate([own_key, own_value], axis=1), "ctx", axis=0, tiled=True
    )
    summary_key, summary_value = summary[:, :col_count], summary[:, col_count:]
    total_blocks = summary_key.shape[0]
    summary_key = summary_key.reshape(total_blocks, head_count, HDIM)
    summary_value = summary_value.reshape(total_blocks, head_count, HDIM)
    first_block = lax.axis_index("ctx") * blocks
    query_ids = first_block + jnp.arange(blocks, dtype=jnp.int32)
    own_doc = lax.dynamic_slice_in_dim(block_doc, first_block, blocks, 0)
    block_ids = jnp.arange(total_blocks, dtype=jnp.int32)
    allowed = (block_ids[None, :] < query_ids[:, None]) & (block_doc[None, :] == own_doc[:, None])
    positions = jnp.arange(BLOCK, dtype=jnp.int32)
    causal = positions[None, :] <= positions[:, None]
    combined_output, local_weight, distant_weight = attend(
        query_row_matrix,
        key_row_matrix,
        value_row_matrix,
        summary_key,
        summary_value,
        allowed,
        causal,
        score_scale_factor,
    )
    attn = combined_output.reshape(tok_rows, col_count)
    partial_value = jnp.dot(attn, w_out, preferred_element_type=jnp.float32)
    summed = scatter_sum(partial_value, "tp")
    shard_width = summed.shape[1]
    residual = lax.dynamic_slice_in_dim(tokens, lax.axis_index("tp") * shard_width, shard_width, 1)
    output = (residual.astype(jnp.float32) + summed).astype(jnp.bfloat16)
    upstream_full = lax.all_gather(grad_out, "tp", axis=1, tiled=True)
    d_attn = back_project(upstream_full, w_out).astype(jnp.bfloat16)
    grads = attend_back(
        query_row_matrix,
        key_row_matrix,
        value_row_matrix,
        summary_key,
        summary_value,
        combined_output,
        local_weight,
        distant_weight,
        d_attn.reshape(block_shape),
        score_scale_factor,
    )
    query_gradient, d_key, d_value, summary_key_gradient, summary_value_gradient = grads
    flat_key = summary_key_gradient.reshape(total_blocks, col_count)
    flat_value = summary_value_gradient.reshape(total_blocks, col_count)
    back = lax.psum_scatter(
        jnp.concatenate([flat_key, flat_value], axis=1), "ctx", scatter_dimension=0, tiled=True
    )
    back_key, back_value = back[:, :col_count], back[:, col_count:]
    query_gradient = query_gradient.astype(jnp.bfloat16).reshape(tok_rows, col_count)
    d_key = (
        d_key.at[:, BLOCK - 1]
        .add(back_key.reshape(blocks, head_count, HDIM))
        .astype(jnp.bfloat16)
        .reshape(tok_rows, col_count)
    )
    d_value = (
        d_value.at[:, BLOCK - 1]
        .add(back_value.reshape(blocks, head_count, HDIM))
        .astype(jnp.bfloat16)
        .reshape(tok_rows, col_count)
    )
    d_partial = (
        back_project(query_gradient, w_query)
        + back_project(d_key, w_key)
        + back_project(d_value, w_value)
    )
    d_summed = scatter_sum(d_partial, "tp")
    grad_tokens = (grad_out.astype(jnp.float32) + d_summed).astype(jnp.bfloat16)
    stacked = jnp.concatenate([query_gradient, d_key, d_value], axis=1)
    joined = lax.psum_scatter(
        term_maker(tokens, stacked).astype(jnp.bfloat16), "ctx", scatter_dimension=0, tiled=True
    ).astype(jnp.float32)
    grad_query_weight = joined[:, :col_count]
    grad_key_weight = joined[:, col_count : 2 * col_count]
    grad_value_weight = joined[:, 2 * col_count :]
    out_term = lax.dot_general(
        attn, upstream_full, (((0,), (0,)), ((), ())), preferred_element_type=jnp.float32
    )
    grad_out_weight = lax.psum_scatter(
        out_term.astype(jnp.bfloat16), "ctx", scatter_dimension=1, tiled=True
    ).astype(jnp.float32)
    return (
        output,
        grad_tokens,
        grad_query_weight,
        grad_key_weight,
        grad_value_weight,
        grad_out_weight,
    )


def solution(mesh):
    in_specs = (
        P("ctx", None),
        P(None, "tp"),
        P(None, "tp"),
        P(None, "tp"),
        P("tp", None),
        P(),
        P("ctx", "tp"),
    )
    out_specs = (
        P("ctx", "tp"),
        P("ctx", "tp"),
        P("ctx", "tp"),
        P("ctx", "tp"),
        P("ctx", "tp"),
        P("tp", "ctx"),
    )
    return jax.shard_map(
        per_device, mesh=mesh, in_specs=in_specs, out_specs=out_specs, check_vma=False
    )
```

profile of v0, /device:TPU:0, one launch (start us, length us, event | category | flops | bytes accessed | tf_op | source)
XLA Modules:
  0.0 398.4 jit_solution(12532342592921492758)
XLA Ops:
  8.0 9.3 %fusion.14 = bf16[64,8,8,128]{3,1,2,0:T(8,128)(2,1)S(1)} fusion(bf16[512,4096]{1,0:T(8,128)(2,1)} %param.11, bf16[4096,1024]{1,0:T(8,128)(2,1)} %param.12), kind=kOutput, calls=%fused_computation.41 | convolution fusion | flops 4295491584 | bytes 13631488 | tf_op jit(solution)/shard_map/dot_general | solution.py:132
  17.3 4.5 %fusion.15 = bf16[64,8,8,128]{3,1,2,0:T(8,128)(2,1)S(1)} fusion(bf16[512,4096]{1,0:T(8,128)(2,1)S(1)} %copy-done.18, bf16[4096,1024]{1,0:T(8,128)(2,1)S(1)} %copy-done.27), kind=kOutput, calls=%fused_computation.42 | convolution fusion | flops 4295491584 | bytes 13631488 | tf_op jit(solution)/shard_map/dot_general | solution.py:132
  22.3 9.5 %fusion.13 = bf16[64,8,8,128]{3,1,2,0:T(8,128)(2,1)S(1)} fusion(bf16[512,4096]{1,0:T(8,128)(2,1)} %param.11, bf16[4096,1024]{1,0:T(8,128)(2,1)} %param.14), kind=kOutput, calls=%fused_computation.40 | convolution fusion | flops 4295491584 | bytes 13631488 | tf_op jit(solution)/shard_map/dot_general | solution.py:132
  32.2 0.9 copy-done.12
  33.2 11.3 %all_gather.6 = bf16[64,2048]{1,0:T(8,128)(2,1)S(1)} all-gather(bf16[8,2048]{1,0:T(8,128)(2,1)S(1)} %pad_maximum_fusion.1), channel_id=1, replica_groups=mesh['ctx'=8,'tp'=4] {'ctx'}, dimensions={0}, use_global_device_ids=true | all-gather | bytes 294912 | tf_op jit(solution)/shard_map/all_gather | solution.py:139
  44.8 1.2 fusion.51
  49.2 2.1 fusion.29
  51.3 41.8 %all-gather.2.cloned.1.call-done = bf16[512,4096]{1,0:T(8,128)(2,1)} async-done(((bf16[512,1024]{1,0:T(8,128)(2,1)}), bf16[512,4096]{1,0:T(8,128)(2,1)}) %all-gather.2.cloned.1.call-update) | async-done | bytes 4194320 | tf_op jit(solution)/shard_map/all_gather | solution.py:169
  93.0 9.2 %fusion.16 = bf16[64,8,8,128]{3,1,2,0:T(8,128)(2,1)S(1)} fusion(bf16[512,4096]{1,0:T(8,128)(2,1)} %all-gather.2.cloned.1.call-done, bf16[1024,4096]{1,0:T(8,128)(2,1)} %param.15), kind=kOutput, calls=%fused_computation.43 | convolution fusion | flops 4295491584 | bytes 13631488 | tf_op jit(solution)/shard_map/dot_general | solution.py:96
  103.0 0.8 copy-done.11
  103.8 1.1 multiply_reduce_fusion
  104.9 1.7 copy.123
  106.6 1.1 fusion.8
  107.8 1.0 copy-done.5
  109.4 0.9 pad_maximum_fusion
  110.3 9.0 %convolution_convert_fusion = bf16[1024,4096]{1,0:T(8,128)(2,1)} fusion(bf16[512,4096]{1,0:T(8,128)(2,1)} %all-gather.2.cloned.1.call-done, bf16[64,8,8,128]{3,2,1,0:T(8,128)(2,1)S(1)} %bitcast.187), kind=kOutput, calls=%fused_computation.2 | convolution fusion | flops 4299161600 | bytes 13631488 | tf_op jit(solution)/shard_map/dot_general | solution.py:217
  120.1 2.4 fusion.39
  122.6 1.3 copy-done.8
  123.9 1.0 multiply_convert_fusion
  127.6 1.0 copy-done.2
  128.5 1.2 copy.258
  130.2 12.8 %reduce-scatter.4.cloned.1.call-done = f32[8,2048]{1,0:T(8,128)} async-done(((f32[64,2048]{1,0:T(8,128)}), f32[8,2048]{1,0:T(8,128)}) %reduce-scatter.4.cloned.1.call-update) | async-done | bytes 65552 | tf_op jit(solution)/shard_map/reduce_scatter | solution.py:186
  143.8 1.7 scatter-add.9
  145.5 1.8 convert_element_type.135
  147.3 1.7 copy.144
  151.2 1.4 copy-done.19
  153.3 18.2 %convert_bitcast_fusion = bf16[4096,3072]{0,1:T(8,128)(2,1)} fusion(bf16[512,4096]{1,0:T(8,128)(2,1)S(1)} %copy-done.19, bf16[512,1024]{1,0:T(8,128)(2,1)S(1)} %bitcast.191, bf16[512,1024]{1,0:T(8,128)(2,1)S(1)} %bitcast.190, bf16[512,1024]{1,0:T(8,128)(2,1)S(1)} %bitcast.189), kind=kOutput, calls=%fused_computation | convolution fusion | flops 12906921984 | bytes 32505856 | tf_op jit(solution)/shard_map/dot_general | solution.py:102
  171.6 1.3 copy-done.16
  173.0 10.1 %fusion.20 = f32[512,4096]{1,0:T(8,128)} fusion(bf16[1024,4096]{1,0:T(8,128)(2,1)} %param.15, bf16[64,8,8,128]{3,2,1,0:T(8,128)(2,1)S(1)} %bitcast.188), kind=kOutput, calls=%fused_computation.52 | convolution fusion | flops 4294967296 | bytes 17825792 | tf_op jit(solution)/shard_map/dot_general | solution.py:164
  183.0 5.0 %dynamic-slice_convert_fusion.5 = (bf16[512,1024]{1,0:T(8,128)(2,1)}, bf16[512,1024]{1,0:T(8,128)(2,1)}, bf16[512,1024]{1,0:T(8,128)(2,1)}) fusion(f32[512,4096]{1,0:T(8,128)} %fusion.20, s32[]{:T(128)S(6)} %select_n.64, s32[]{:T(128)S(6)} %select_n.68, s32[]{:T(128)S(6)} %select_n.66), kind=kLoop, calls=%fused_computation.27 | loop fusion | bytes 6291468 | tf_op jit(solution)/shard_map/convert_element_type | solution.py:118
  188.1 1.3 collective-permute-start
  189.4 2.8 collective-permute-start.2
  192.5 10.5 %fusion.48 = f32[512,4096]{1,0:T(8,128)} fusion(bf16[4096,1024]{1,0:T(8,128)(2,1)} %param.12, bf16[64,8,8,128]{3,2,1,0:T(8,128)(2,1)S(1)} %bitcast.178), kind=kOutput, calls=%fused_computation.104 | convolution fusion | flops 4294967296 | bytes 17825792 | tf_op jit(solution)/shard_map/dot_general | solution.py:96
  203.0 6.8 %fusion.49 = f32[512,4096]{1,0:T(8,128)} fusion(bf16[4096,1024]{1,0:T(8,128)(2,1)S(1)} %bitcast.200, bf16[64,8,8,128]{3,2,1,0:T(8,128)(2,1)S(1)} %bitcast.182), kind=kOutput, calls=%fused_computation.105 | convolution fusion | flops 4294967296 | bytes 17825792 | tf_op jit(solution)/shard_map/dot_general | solution.py:96
  209.8 12.9 %add_add_fusion = f32[512,4096]{1,0:T(8,128)} fusion(f32[512,4096]{1,0:T(8,128)} %fusion.48, f32[512,4096]{1,0:T(8,128)} %fusion.49, bf16[4096,1024]{1,0:T(8,128)(2,1)} %param.14, bf16[64,8,8,128]{3,2,1,0:T(8,128)(2,1)S(1)} %bitcast.180), kind=kOutput, calls=%fused_computation.1 | convolution fusion | flops 4299161600 | bytes 34603008 | tf_op jit(solution)/shard_map/dot_general | solution.py:96
  222.7 4.3 %dynamic-slice_convert_fusion.2 = (bf16[512,1024]{1,0:T(8,128)(2,1)}, bf16[512,1024]{1,0:T(8,128)(2,1)S(1)}, bf16[512,1024]{1,0:T(8,128)(2,1)S(1)}) fusion(f32[512,4096]{1,0:T(8,128)} %add_add_fusion, s32[]{:T(128)S(6)} %select_n.64, s32[]{:T(128)S(6)} %select_n.68, s32[]{:T(128)S(6)} %select_n.66), kind=kLoop, calls=%fused_computation.20 | loop fusion | bytes 6291468 | tf_op jit(solution)/shard_map/convert_element_type | solution.py:118
  227.0 1.4 collective-permute-start.3
  228.4 2.4 collective-permute-start.5
  230.8 30.7 %collective-permute-start.4 = (bf16[512,1024]{1,0:T(8,128)(2,1)S(1)}, bf16[512,1024]{1,0:T(8,128)(2,1)}, u32[]{:S(2)}, u32[]{:S(2)}) collective-permute-start(bf16[512,1024]{1,0:T(8,128)(2,1)S(1)} %get-tuple-element.56), channel_id=1, source_target_pairs={{0,2},{1,3},{2,0},{3,1},{4,6},{5,7},{6,4},{7,5},{8,10},{9,11},{10,... | collective-permute-start | bytes 3145736 | tf_op jit(solution)/shard_map/ppermute | solution.py:118
  261.5 44.7 %collective-permute-done.1 = bf16[512,1024]{1,0:T(8,128)(2,1)} collective-permute-done((bf16[512,1024]{1,0:T(8,128)(2,1)}, bf16[512,1024]{1,0:T(8,128)(2,1)}, u32[]{:S(2)}, u32[]{:S(2)}) %collective-permute-start.1) | collective-permute-done | bytes 1048608 | tf_op jit(solution)/shard_map/ppermute | solution.py:118
  306.2 4.8 %add_convert_fusion.1 = bf16[512,1024]{1,0:T(8,128)(2,1)} fusion(bf16[512,1024]{1,0:T(8,128)(2,1)} %collective-permute-done.2, bf16[512,1024]{1,0:T(8,128)(2,1)} %collective-permute-done.1, bf16[512,1024]{1,0:T(8,128)(2,1)} %collective-permute-done, f32[512,4096]{1,0:T(8,128)} %fusion.20, s32[]{:T(128)S(6)} %select_n.62, bf16[512,4096]{1,0:T(8,128)(2,1)} %param.11, ...), kind=kLoop, calls=%fused_computation.24 | loop fusion | flops 4718592 | bytes 7340040 | tf_op jit(solution)/shard_map/convert_element_type | solution.py:168
  311.0 60.6 %collective-permute-done.4 = bf16[512,1024]{1,0:T(8,128)(2,1)} collective-permute-done((bf16[512,1024]{1,0:T(8,128)(2,1)S(1)}, bf16[512,1024]{1,0:T(8,128)(2,1)}, u32[]{:S(2)}, u32[]{:S(2)}) %collective-permute-start.4) | collective-permute-done | bytes 1048608 | tf_op jit(solution)/shard_map/ppermute | solution.py:118
  371.5 4.6 %add_convert_fusion = bf16[512,1024]{1,0:T(8,128)(2,1)} fusion(bf16[512,1024]{1,0:T(8,128)(2,1)} %collective-permute-done.5, bf16[512,1024]{1,0:T(8,128)(2,1)} %collective-permute-done.4, bf16[512,1024]{1,0:T(8,128)(2,1)} %collective-permute-done.3, f32[512,4096]{1,0:T(8,128)} %add_add_fusion, s32[]{:T(128)S(6)} %select_n.62, bf16[512,1024]{1,0:T(8,128)(2,1)S(1)} %copy-done.7), kind=kLoop, calls=%fused_computation.17 | loop fusion | flops 4718592 | bytes 7340036 | tf_op jit(solution)/shard_map/convert_element_type | solution.py:209
  376.2 2.9 convert_element_type.147
  379.1 4.8 %fusion.50 = (f32[512,1024]{0,1:T(8,128)}, f32[512,1024]{0,1:T(8,128)}, f32[512,1024]{0,1:T(8,128)S(1)}) fusion(bf16[512,3072]{0,1:T(8,128)(2,1)} %reduce-scatter.6.cloned.1.call-done), kind=kLoop, calls=%fused_computation.106 | loop fusion | bytes 12582912 | tf_op jit(solution)/shard_map/slice | solution.py:216
  383.8 2.9 copy.147
  386.7 2.9 copy.146
  389.6 1.8 copy.145
  (113 shorter events, 14.5 us)
Async XLA Ops:
  7.2 85.9 %all-gather.2.cloned.1.call-start = ((), (), s32[]{:S(2)}) async-start(), calls=%async_computation.3 | async-start | bytes 5242880 | tf_op jit(solution)/shard_map/all_gather | solution.py:169
  7.9 135.1 %reduce-scatter.4.cloned.1.call-start = ((), (), s32[]{:S(2)}) async-start(), calls=%async_computation.4 | async-start | bytes 589824 | tf_op jit(solution)/shard_map/reduce_scatter | solution.py:186
  7.9 9.3 %copy-start.18 = (bf16[512,4096]{1,0:T(8,128)(2,1)S(1)}, bf16[512,4096]{1,0:T(8,128)(2,1)}, u32[]{:S(2)}) copy-start(bf16[512,4096]{1,0:T(8,128)(2,1)} %param.11) | copy-start | bytes 12582916
  8.0 9.3 %copy-start.27 = (bf16[4096,1024]{1,0:T(8,128)(2,1)S(1)}, bf16[4096,1024]{1,0:T(8,128)(2,1)}, u32[]{:S(2)}) copy-start(bf16[4096,1024]{1,0:T(8,128)(2,1)} %param.13) | copy-start | bytes 25165828
  22.3 23.6 %copy-start = (bf16[64,8,8,128]{3,2,1,0:T(8,128)(2,1)}, bf16[64,8,8,128]{3,2,1,0:T(8,128)(2,1)S(1)}, u32[]{:S(2)}) copy-start(bf16[64,8,8,128]{3,2,1,0:T(8,128)(2,1)S(1)} %copy.169) | copy-start | bytes 3145732
  31.9 12.7 %copy-start.26 = (s32[64]{0:T(128)S(1)}, s32[64]{0:T(128)}, u32[]{:S(2)}) copy-start(s32[64]{0:T(128)} %param.16) | copy-start | bytes 772
  32.2 1.0 copy-start.12
  46.6 1.9 copy-start.9
  47.3 1.3 copy-start.20
  47.9 1.2 copy-start.13
  48.0 0.6 copy-start.24
  102.2 1.6 copy-start.11
  104.9 2.8 copy-start.22
  107.7 1.0 copy-start.5
  108.7 1.6 copy-start.15
  110.2 265.9 %reduce-scatter.8.cloned.1.call-start = ((), (), s32[]{:S(2)}) async-start(), calls=%async_computation.6 | async-start | bytes 9437184 | tf_op jit(solution)/shard_map/reduce_scatter | solution.py:220
  119.3 0.8 copy-start.21
  119.3 0.8 copy-start.25
  119.3 4.5 %copy-start.14 = (bf16[64,8,8,128]{3,2,1,0:T(8,128)(2,1)S(1)}, bf16[64,8,8,128]{3,2,1,0:T(8,128)(2,1)}, u32[]{:S(2)}) copy-start(bf16[64,8,8,128]{3,2,1,0:T(8,128)(2,1)} %copy-done.12) | copy-start | bytes 3145732
  119.3 4.5 %copy-start.23 = (f32[8,64,8]{1,2,0:T(8,128)S(1)}, f32[8,64,8]{1,2,0:T(8,128)}, u32[]{:S(2)}) copy-start(f32[8,64,8]{1,2,0:T(8,128)} %copy-done.22) | copy-start | bytes 49156
  119.4 259.7 %reduce-scatter.6.cloned.1.call-start = ((), (), s32[]{:S(2)}) async-start(), calls=%async_computation.5 | async-start | bytes 28311552 | tf_op jit(solution)/shard_map/reduce_scatter | solution.py:211
  120.1 3.8 copy-start.10
  122.5 1.3 copy-start.8
  123.8 1.2 copy-start.1
  125.1 1.2 copy-start.6
  127.5 1.0 copy-start.2
  149.7 1.2 copy-start.4
  149.7 2.9 copy-start.19
  150.4 2.9 copy-start.17
  171.6 1.4 copy-start.16
  183.0 9.5 %copy-start.3 = (bf16[8,64,8,128]{3,2,1,0:T(8,128)(2,1)S(1)}, bf16[8,64,8,128]{3,2,1,0:T(8,128)(2,1)}, u32[]{:S(2)}) copy-start(bf16[8,64,8,128]{3,2,1,0:T(8,128)(2,1)} %copy-done.2) | copy-start | bytes 3145732
  188.1 42.8 %collective-permute-start = (bf16[512,1024]{1,0:T(8,128)(2,1)}, bf16[512,1024]{1,0:T(8,128)(2,1)}, u32[]{:S(2)}, u32[]{:S(2)}) collective-permute-start(bf16[512,1024]{1,0:T(8,128)(2,1)} %get-tuple-element.57), channel_id=1, source_target_pairs={{0,1},{1,2},{2,3},{3,0},{4,5},{5,6},{6,7},{7,4},{8,9},{9,10},{10,1... | collective-permute-start | bytes 3145736 | tf_op jit(solution)/shard_map/ppermute | solution.py:118
  189.4 72.1 %collective-permute-start.2 = (bf16[512,1024]{1,0:T(8,128)(2,1)}, bf16[512,1024]{1,0:T(8,128)(2,1)}, u32[]{:S(2)}, u32[]{:S(2)}) collective-permute-start(bf16[512,1024]{1,0:T(8,128)(2,1)} %get-tuple-element.58), channel_id=1, source_target_pairs={{0,3},{1,0},{2,1},{3,2},{4,7},{5,4},{6,5},{7,6},{8,11},{9,8},{10,9... | collective-permute-start | bytes 3145736 | tf_op jit(solution)/shard_map/ppermute | solution.py:118
  192.1 10.9 %slice-start = ((s8[8388608]{0:T(1024)(128)(4,1)}), s8[4194304]{0:T(1024)(128)(4,1)S(1)}, s32[]{:S(2)}) async-start(s8[8388608]{0:T(1024)(128)(4,1)} %bitcast.199), calls=%async_computation.7 | async-start | bytes 8388608
  192.1 10.9 %slice-start.1 = ((s8[8388608]{0:T(1024)(128)(4,1)}), s8[4194304]{0:T(1024)(128)(4,1)S(1)}, s32[]{:S(2)}) async-start(s8[8388608]{0:T(1024)(128)(4,1)} %bitcast.199), calls=%async_computation.8 | async-start | bytes 8388608
  192.1 114.1 %collective-permute-start.1 = (bf16[512,1024]{1,0:T(8,128)(2,1)}, bf16[512,1024]{1,0:T(8,128)(2,1)}, u32[]{:S(2)}, u32[]{:S(2)}) collective-permute-start(bf16[512,1024]{1,0:T(8,128)(2,1)} %get-tuple-element.59), channel_id=1, source_target_pairs={{0,2},{1,3},{2,0},{3,1},{4,6},{5,7},{6,4},{7,5},{8,10},{9,11},{10,... | collective-permute-start | bytes 3145736 | tf_op jit(solution)/shard_map/ppermute | solution.py:118
  227.0 84.0 %collective-permute-start.3 = (bf16[512,1024]{1,0:T(8,128)(2,1)}, bf16[512,1024]{1,0:T(8,128)(2,1)}, u32[]{:S(2)}, u32[]{:S(2)}) collective-permute-start(bf16[512,1024]{1,0:T(8,128)(2,1)} %get-tuple-element.54), channel_id=1, source_target_pairs={{0,1},{1,2},{2,3},{3,0},{4,5},{5,6},{6,7},{7,4},{8,9},{9,10},{10,1... | collective-permute-start | bytes 3145736 | tf_op jit(solution)/shard_map/ppermute | solution.py:118
  228.4 82.6 %collective-permute-start.5 = (bf16[512,1024]{1,0:T(8,128)(2,1)S(1)}, bf16[512,1024]{1,0:T(8,128)(2,1)}, u32[]{:S(2)}, u32[]{:S(2)}) collective-permute-start(bf16[512,1024]{1,0:T(8,128)(2,1)S(1)} %get-tuple-element.55), channel_id=1, source_target_pairs={{0,3},{1,0},{2,1},{3,2},{4,7},{5,4},{6,5},{7,6},{8,11},{9,8},{10,9... | collective-permute-start | bytes 3145736 | tf_op jit(solution)/shard_map/ppermute | solution.py:118
  230.8 140.7 %collective-permute-start.4 = (bf16[512,1024]{1,0:T(8,128)(2,1)S(1)}, bf16[512,1024]{1,0:T(8,128)(2,1)}, u32[]{:S(2)}, u32[]{:S(2)}) collective-permute-start(bf16[512,1024]{1,0:T(8,128)(2,1)S(1)} %get-tuple-element.56), channel_id=1, source_target_pairs={{0,2},{1,3},{2,0},{3,1},{4,6},{5,7},{6,4},{7,5},{8,10},{9,11},{10,... | collective-permute-start | bytes 3145736 | tf_op jit(solution)/shard_map/ppermute | solution.py:118
  261.5 110.0 %copy-start.7 = (bf16[512,1024]{1,0:T(8,128)(2,1)S(1)}, bf16[512,1024]{1,0:T(8,128)(2,1)}, u32[]{:S(2)}) copy-start(bf16[512,1024]{1,0:T(8,128)(2,1)} %param.17) | copy-start | bytes 3145732
Sparse Core Ops, SparseCore 0:
  9.5 83.4 all-gather.1
  110.4 32.5 reduce-scatter.3
  146.5 71.3 reduce-scatter.7
  221.3 155.9 reduce-scatter.5
where the time goes:
time: 406 us; the launch traced here: 398 us
  waiting for transfers between devices  161 us (40%)
  matrix products  112 us (28%)
  local copies, waits for them, and re-layouts  43.5 us (11%)
  starting transfers between devices  39.1 us (10%)
  other arithmetic  17.1 us (4%)
  between operations  14.8 us (4%)
  blocking collectives  11.3 us (3%)
    ppermute x6, waiting for transfers between devices, scatter_sum(): moved = lax.ppermute(block(shift).astype(jnp.bfloat16), axis, ring)  105 us
    all_gather x1, waiting for transfers between devices, per_device(): upstream_full = lax.all_gather(grad_out, 'tp', axis=1, tiled=True)  41.8 us
    dot_general x4, matrix products, back_project(): lax.dot_general(grad_rows, weight, (((1,), (1,)), ((), ())), preferred_el...  39.3 us
    ppermute x6, starting transfers between devices, scatter_sum(): moved = lax.ppermute(block(shift).astype(jnp.bfloat16), axis, ring)  39 us
    dot_general x3, matrix products, project(): jnp.dot(tokens, weight, preferred_element_type=jnp.float32)  23.3 us
    unnamed x76, local copies, waits for them, and re-layouts  22.3 us
    dot_general x1, matrix products, term_maker(): lax.dot_general(tokens, grad_rows, (((0,), (0,)), ((), ())), preferred_el...  18.2 us
    reduce_scatter x1, waiting for transfers between devices, per_device(): lax.psum_scatter(jnp.concatenate([flat_key, flat_value], axis=1), 'ctx',...  12.8 us
  transfers between devices with their start and end apart: 10, of which 4 were waited for; matrix products, arithmetic and copies ran while one was open for 34% of the time, Pallas kernels for 0%

commit v1 on v0

--- a/solution.py
+++ b/solution.py
@@ -1,13 +1,18 @@
+import functools
 import math
 
 import jax
 import jax.numpy as jnp
 from jax import lax
+from jax.experimental import pallas as pl
+from jax.experimental.pallas import tpu as pltpu
 from jax.sharding import PartitionSpec as P
 
 HDIM = 128
 BLOCK = 64
-
+HALF = 128
+
+MESH = pl.DeviceIdType.MESH
 
 big_negative = -1e30
 
@@ -98,13 +103,7 @@
     )
 
 
-def term_maker(tokens, grad_rows):
-    return lax.dot_general(
-        tokens, grad_rows, (((0,), (0,)), ((), ())), preferred_element_type=jnp.float32
-    )
-
-
-def scatter_sum(partial, axis):
+def column_pieces(partial, axis):
     count = lax.axis_size(axis)
     me = lax.axis_index(axis)
     width = partial.shape[1] // count
@@ -112,12 +111,312 @@
     def block(shift):
         return lax.dynamic_slice_in_dim(partial, ((me + shift) % count) * width, width, 1)
 
-    total = block(0)
+    return [block(0)] + [block(shift).astype(jnp.bfloat16) for shift in range(1, count)]
+
+
+def send_pieces(pieces, axis):
+    count = lax.axis_size(axis)
+    return [
+        lax.ppermute(pieces[shift], axis, [(source, (source + shift) % count) for source in range(count)])
+        for shift in range(1, count)
+    ]
+
+
+def tail_kernel(names, cbits, tbits, per, *refs):
+    turned_ref, dq_ref, dk_ref, dv_ref, edge_ref, land_ref = refs[:6]
+    wq_ref, wk_ref, wv_ref, gout_ref, out_ref, tok_ref = refs[6:12]
+    scratch = list(refs[12:])
+    grad_ref, weight_buf, total_ref, landed_ref = scratch[:4]
+    sent, landed = scratch[4 : 4 + cbits], scratch[4 + cbits : 4 + 2 * cbits]
+    scratch = scratch[4 + 2 * cbits :]
+    tsent, tlanded = scratch[:tbits], scratch[tbits : 2 * tbits]
+    load_sem, weight_sem, land_send, land_recv, send_sem, recv_sem, tsend, trecv = scratch[
+        2 * tbits :
+    ]
+    axis, other_axis = names
+    count, tiles, slots = 1 << cbits, landed[0].shape[0], sent[0].shape[0]
+    rows = out_ref.shape[1]
+    length, width = tok_ref.shape
+    sub_width = weight_buf.shape[2]
+    subs = width // sub_width
+    edge_rows = edge_ref.shape[1]
+    me, other_me = lax.axis_index(axis), lax.axis_index(other_axis)
+    digit = [(me // (1 << b)) % 2 for b in range(cbits)]
+    partner = [me + (1 - 2 * digit[b]) * (1 << b) for b in range(cbits)]
+    tdigit = [(other_me // (1 << b)) % 2 for b in range(tbits)]
+    tpartner = [other_me + (1 - 2 * tdigit[b]) * (1 << b) for b in range(tbits)]
+    rest = list(range(1, cbits))
+    orders = ([0] + rest, [0] + rest[::-1])
+
+    loads = [
+        pltpu.make_async_copy(ref, grad_ref.at[w], load_sem.at[w])
+        for w, ref in enumerate((dq_ref, dk_ref, dv_ref))
+    ]
+    for load in loads:
+        load.start()
+
+    barrier = pltpu.get_barrier_semaphore()
     for shift in range(1, count):
-        ring = [(source, (source + shift) % count) for source in range(count)]
-        moved = lax.ppermute(block(shift).astype(jnp.bfloat16), axis, ring)
-        total = total + moved.astype(jnp.float32)
-    return total
+        pl.semaphore_signal(
+            barrier, inc=1, device_id={axis: (me + shift) % count}, device_id_type=MESH
+        )
+    for b in range(tbits):
+        pl.semaphore_signal(
+            barrier, inc=1, device_id={other_axis: tpartner[b]}, device_id_type=MESH
+        )
+    pl.semaphore_wait(barrier, count - 1 + tbits)
+
+    def land_copy(shift):
+        peer = (me + shift) % count
+        return pltpu.make_async_remote_copy(
+            src_ref=land_ref.at[pl.ds(pl.multiple_of(peer * edge_rows, edge_rows), edge_rows), :],
+            dst_ref=landed_ref.at[shift - 1],
+            send_sem=land_send.at[shift - 1],
+            recv_sem=land_recv.at[shift - 1],
+            device_id={axis: peer},
+            device_id_type=MESH,
+        )
+
+    for shift in range(1, count):
+        land_copy(shift).start()
+
+    def copy(tile, half, stage):
+        return pltpu.make_async_remote_copy(
+            src_ref=sent[stage].at[tile % slots, half],
+            dst_ref=landed[stage].at[tile, half],
+            send_sem=send_sem.at[stage, tile, half],
+            recv_sem=recv_sem.at[stage, tile, half],
+            device_id={axis: partner[orders[half][stage]]},
+            device_id_type=MESH,
+        )
+
+    def tcopy(stage, at):
+        return pltpu.make_async_remote_copy(
+            src_ref=tsent[stage].at[at],
+            dst_ref=tlanded[stage].at[at],
+            send_sem=tsend.at[stage, at],
+            recv_sem=trecv.at[stage, at],
+            device_id={other_axis: tpartner[stage]},
+            device_id_type=MESH,
+        )
+
+    def product(row_block, tile, half):
+        which = tile // per
+        start = pl.multiple_of((tile % per) * 2 * HALF + half * HALF, HALF)
+        left = turned_ref[pl.ds(pl.multiple_of(row_block * rows, rows), rows), :]
+        return jnp.dot(
+            left, grad_ref[which, :, pl.ds(start, HALF)], preferred_element_type=jnp.float32
+        )
+
+    def stage_step(tile, stage):
+        for half in (0, 1):
+            order = orders[half]
+            if stage:
+                copy(tile, half, stage - 1).wait_recv()
+            if stage < cbits:
+
+                @pl.when(tile >= slots)
+                def _():
+                    copy(tile - slots, half, stage).wait_send()
+
+            for r in range(1 << max(cbits - 1 - stage, 0)):
+                if stage == cbits:
+                    row_block = me
+                else:
+                    b = order[stage]
+                    row_block = (1 - digit[b]) * (1 << b)
+                    for i in range(stage):
+                        row_block += digit[order[i]] * (1 << order[i])
+                    for i in range(stage + 1, cbits):
+                        row_block += ((r >> (cbits - 1 - i)) & 1) * (1 << order[i])
+                value = product(row_block, tile, half)
+                for t in range(stage):
+                    at = r
+                    for i in range(t + 1, min(stage, cbits)):
+                        at += digit[order[i]] * (1 << (cbits - 1 - i))
+                    if stage < cbits:
+                        at += (1 - digit[order[stage]]) * (1 << (cbits - 1 - stage))
+                    value += landed[t][tile, half, at].astype(jnp.float32)
+                if stage < cbits:
+                    sent[stage][tile % slots, half, r] = value.astype(jnp.bfloat16)
+                else:
+                    start = pl.multiple_of((tile % per) * 2 * HALF + half * HALF, HALF)
+                    out_ref[tile // per, :, pl.ds(start, HALF)] = value
+            if stage < cbits:
+                copy(tile, half, stage).start()
+
+    bases = [0]
+    for stage in range(tbits):
+        bases.append(bases[-1] + subs * (1 << (tbits - 1 - stage)))
+    bases.append(bases[-1] + subs)
+    turns = bases[-1]
+
+    def weight_loads(k, stage):
+        inside = k - bases[stage]
+        r, sub = inside // subs, inside % subs
+        if stage == tbits:
+            block = other_me
+        else:
+            block = (1 - tdigit[stage]) * (1 << stage)
+            for i in range(stage):
+                block += tdigit[i] * (1 << i)
+            for i in range(stage + 1, tbits):
+                block += ((r // (1 << (tbits - 1 - i))) % 2) * (1 << i)
+        start = pl.multiple_of(block * width + sub * sub_width, sub_width)
+        return [
+            pltpu.make_async_copy(
+                ref.at[pl.ds(start, sub_width), :], weight_buf.at[k % 2, w], weight_sem.at[k % 2, w]
+            )
+            for w, ref in enumerate((wq_ref, wk_ref, wv_ref))
+        ]
+
+    def fetch(k):
+        for stage in range(tbits + 1):
+
+            @pl.when((k >= bases[stage]) & (k < bases[stage + 1]))
+            def _():
+                for load in weight_loads(k, stage):
+                    load.start()
+
+    def turn(k):
+        for load in weight_loads(k, 0):
+            load.wait()
+        fetch(k + 1)
+        value = None
+        for w in range(3):
+            term = lax.dot_general(
+                grad_ref[w],
+                weight_buf[k % 2, w],
+                (((1,), (1,)), ((), ())),
+                preferred_element_type=jnp.float32,
+            )
+            value = term if value is None else value + term
+        total_ref[...] = value
+        for stage in range(tbits + 1):
+
+            @pl.when((k >= bases[stage]) & (k < bases[stage + 1]))
+            def _():
+                inside = k - bases[stage]
+                result = total_ref[...]
+                for t in range(stage):
+                    at = inside // subs
+                    for i in range(t + 1, min(stage, tbits)):
+                        at += tdigit[i] * (1 << (tbits - 1 - i))
+                    if stage < tbits:
+                        at += (1 - tdigit[stage]) * (1 << (tbits - 1 - stage))
+                    spot = at * subs + inside % subs
+                    tcopy(t, spot).wait_recv()
+                    result += tlanded[t][spot].astype(jnp.float32)
+                if stage < tbits:
+                    tsent[stage][inside] = result.astype(jnp.bfloat16)
+                    tcopy(stage, inside).start()
+                else:
+                    start = pl.multiple_of(inside * sub_width, sub_width)
+                    mine = gout_ref[:, pl.ds(start, sub_width)].astype(jnp.float32)
+                    tok_ref[:, pl.ds(start, sub_width)] = (mine + result).astype(jnp.bfloat16)
+
+    def finish_edges():
+        loads[1].wait()
+        loads[2].wait()
+        for shift in range(1, count):
+            land_copy(shift).wait_recv()
+        columns = edge_ref.shape[2]
+        own = pl.ds(pl.multiple_of(me * edge_rows, edge_rows), edge_rows)
+        for p in (0, 1):
+            part = slice(p * columns, (p + 1) * columns)
+            total = edge_ref[p] + land_ref[own, part]
+            for shift in range(1, count):
+                total += landed_ref[shift - 1, :, part]
+            for j in range(edge_rows):
+                chunk = slice((j + 1) * BLOCK - 16, (j + 1) * BLOCK)
+                old = grad_ref[1 + p, chunk, :].astype(jnp.float32)
+                last = lax.broadcasted_iota(jnp.int32, old.shape, 0) == 15
+                new = jnp.where(last, total[j : j + 1, :], old)
+                grad_ref[1 + p, chunk, :] = new.astype(jnp.bfloat16)
+
+    fetch(0)
+    loads[0].wait()
+    lags = [0] + [2 * s - 1 for s in range(1, cbits + 1)]
+
+    def body(i, carry):
+        for stage in range(cbits, -1, -1):
+            tile = i - lags[stage]
+
+            @pl.when((tile >= 0) & (tile < tiles))
+            def _():
+                stage_step(tile, stage)
+
+        @pl.when(i == 0)
+        def _():
+            finish_edges()
+
+        @pl.when((i >= 1) & (i <= turns))
+        def _():
+            turn(i - 1)
+
+        return carry
+
+    lax.fori_loop(0, max(tiles + lags[cbits], turns + 1), body, 0)
+    for tile in range(max(tiles - slots, 0), tiles):
+        for half in (0, 1):
+            for stage in range(cbits):
+                copy(tile, half, stage).wait_send()
+    for stage in range(tbits):
+        for at in range(tsent[stage].shape[0]):
+            tcopy(stage, at).wait_send()
+    for shift in range(1, count):
+        land_copy(shift).wait_send()
+
+
+def tail(turned, grads, edges, land, weights, grad_out, names, call):
+    axis, other_axis = names
+    count, other_count = lax.axis_size(axis), lax.axis_size(other_axis)
+    cbits, tbits = count.bit_length() - 1, other_count.bit_length() - 1
+    depth, length = turned.shape
+    columns = grads[0].shape[1]
+    width = grad_out.shape[1]
+    rows = depth // count
+    per = columns // (2 * HALF)
+    tiles = 3 * per
+    slots = min(4, tiles)
+    sub_width = min(2 * HALF, width)
+    subs = width // sub_width
+    blocks = [1 << (cbits - 1 - stage) for stage in range(cbits)]
+    tblocks = [subs << (tbits - 1 - stage) for stage in range(tbits)]
+    edge_rows = edges.shape[1]
+    vmem = pl.BlockSpec(memory_space=pltpu.VMEM)
+    hbm = pl.BlockSpec(memory_space=pl.ANY)
+    dma = pltpu.SemaphoreType.DMA
+    return pl.pallas_call(
+        functools.partial(tail_kernel, names, cbits, tbits, per),
+        out_shape=[
+            jax.ShapeDtypeStruct((3, rows, columns), jnp.float32),
+            jax.ShapeDtypeStruct((length, width), jnp.bfloat16),
+        ],
+        in_specs=[vmem, hbm, hbm, hbm, vmem, vmem, hbm, hbm, hbm, vmem],
+        out_specs=[vmem, vmem],
+        scratch_shapes=[
+            pltpu.VMEM((3, length, columns), jnp.bfloat16),
+            pltpu.VMEM((2, 3, sub_width, columns), jnp.bfloat16),
+            pltpu.VMEM((length, sub_width), jnp.float32),
+            pltpu.VMEM((count - 1, edge_rows, 2 * columns), jnp.float32),
+        ]
+        + [pltpu.VMEM((slots, 2, n, rows, HALF), jnp.bfloat16) for n in blocks]
+        + [pltpu.VMEM((tiles, 2, n, rows, HALF), jnp.bfloat16) for n in blocks]
+        + [pltpu.VMEM((n, length, sub_width), jnp.bfloat16) for n in tblocks] * 2
+        + [dma((3,)), dma((2, 3)), dma((count - 1,)), dma((count - 1,))]
+        + [dma((cbits, tiles, 2)), dma((cbits, tiles, 2))]
+        + [dma((tbits, tblocks[0])), dma((tbits, tblocks[0]))],
+        compiler_params=pltpu.CompilerParams(
+            collective_id=call, has_side_effects=True, vmem_limit_bytes=63 * 1024 * 1024
+        ),
+        cost_estimate=pl.CostEstimate(
+            flops=12 * depth * length * columns,
+            bytes_accessed=2 * (depth * length + 3 * length * columns + 3 * depth * columns),
+            transcendentals=0,
+        ),
+        name="tail",
+    )(turned, *grads, edges, land, *weights, grad_out)
 
 
 def per_device(tokens, w_query, w_key, w_value, w_out, block_doc, grad_out):
@@ -127,6 +426,7 @@
     blocks = tok_rows // BLOCK
     head_count = col_count // HDIM
     block_shape = (blocks, BLOCK, head_count, HDIM)
+    upstream_full = lax.all_gather(grad_out, "tp", axis=1, tiled=True)
 
     def project(weight):
         return jnp.dot(tokens, weight, preferred_element_type=jnp.float32).astype(jnp.bfloat16)
@@ -162,11 +462,10 @@
     )
     attn = combined_output.reshape(tok_rows, col_count)
     partial_value = jnp.dot(attn, w_out, preferred_element_type=jnp.float32)
-    summed = scatter_sum(partial_value, "tp")
-    shard_width = summed.shape[1]
-    residual = lax.dynamic_slice_in_dim(tokens, lax.axis_index("tp") * shard_width, shard_width, 1)
-    output = (residual.astype(jnp.float32) + summed).astype(jnp.bfloat16)
-    upstream_full = lax.all_gather(grad_out, "tp", axis=1, tiled=True)
+    turned = tokens.T
+    pieces = column_pieces(partial_value, "tp")
+    upstream_full, pieces, turned = lax.optimization_barrier((upstream_full, pieces, turned))
+    moved = send_pieces(pieces, "tp")
     d_attn = back_project(upstream_full, w_out).astype(jnp.bfloat16)
     grads = attend_back(
         query_row_matrix,
@@ -183,51 +482,37 @@
     query_gradient, d_key, d_value, summary_key_gradient, summary_value_gradient = grads
     flat_key = summary_key_gradient.reshape(total_blocks, col_count)
     flat_value = summary_value_gradient.reshape(total_blocks, col_count)
-    back = lax.psum_scatter(
-        jnp.concatenate([flat_key, flat_value], axis=1), "ctx", scatter_dimension=0, tiled=True
-    )
-    back_key, back_value = back[:, :col_count], back[:, col_count:]
-    query_gradient = query_gradient.astype(jnp.bfloat16).reshape(tok_rows, col_count)
-    d_key = (
-        d_key.at[:, BLOCK - 1]
-        .add(back_key.reshape(blocks, head_count, HDIM))
-        .astype(jnp.bfloat16)
-        .reshape(tok_rows, col_count)
-    )
-    d_value = (
-        d_value.at[:, BLOCK - 1]
-        .add(back_value.reshape(blocks, head_count, HDIM))
-        .astype(jnp.bfloat16)
-        .reshape(tok_rows, col_count)
-    )
-    d_partial = (
-        back_project(query_gradient, w_query)
-        + back_project(d_key, w_key)
-        + back_project(d_value, w_value)
-    )
-    d_summed = scatter_sum(d_partial, "tp")
-    grad_tokens = (grad_out.astype(jnp.float32) + d_summed).astype(jnp.bfloat16)
-    stacked = jnp.concatenate([query_gradient, d_key, d_value], axis=1)
-    joined = lax.psum_scatter(
-        term_maker(tokens, stacked).astype(jnp.bfloat16), "ctx", scatter_dimension=0, tiled=True
-    ).astype(jnp.float32)
-    grad_query_weight = joined[:, :col_count]
-    grad_key_weight = joined[:, col_count : 2 * col_count]
-    grad_value_weight = joined[:, 2 * col_count :]
     out_term = lax.dot_general(
         attn, upstream_full, (((0,), (0,)), ((), ())), preferred_element_type=jnp.float32
     )
     grad_out_weight = lax.psum_scatter(
         out_term.astype(jnp.bfloat16), "ctx", scatter_dimension=1, tiled=True
     ).astype(jnp.float32)
-    return (
-        output,
-        grad_tokens,
-        grad_query_weight,
-        grad_key_weight,
-        grad_value_weight,
-        grad_out_weight,
-    )
+    edges = jnp.stack(
+        [d_key[:, BLOCK - 1].reshape(blocks, col_count), d_value[:, BLOCK - 1].reshape(blocks, col_count)]
+    )
+    rows_of = [
+        part.astype(jnp.bfloat16).reshape(tok_rows, col_count)
+        for part in (query_gradient, d_key, d_value)
+    ]
+    joined, grad_tokens = tail(
+        turned,
+        rows_of,
+        edges,
+        jnp.concatenate([flat_key, flat_value], axis=1),
+        (w_query, w_key, w_value),
+        grad_out,
+        ("ctx", "tp"),
+        0,
+    )
+    joined, moved = lax.optimization_barrier((joined, moved))
+    shard_width = grad_out.shape[1]
+    summed = lax.dynamic_slice_in_dim(tokens, lax.axis_index("tp") * shard_width, shard_width, 1)
+    summed = summed.astype(jnp.float32) + pieces[0]
+    for piece in moved:
+        summed = summed + piece.astype(jnp.float32)
+    output = summed.astype(jnp.bfloat16)
+    return (output, grad_tokens, joined[0], joined[1], joined[2], grad_out_weight)
 
 
 def solution(mesh):

time: 406 us -> 310 us (0.76)
  Pallas kernels: 0 us -> 148 us
  waiting for transfers between devices: 161 us -> 26.9 us
  matrix products: 112 us -> 58.6 us
  starting transfers between devices: 39.1 us -> 3.9 us
  local copies, waits for them, and re-layouts: 43.5 us -> 29.8 us
  other arithmetic: 17.1 us -> 11.8 us
    pallas_call x0 -> x1, Pallas kernels: none -> 148 us  [tail(): pl.pallas_call(functools.partial(tail_kernel, names, cbits, tbits, per),...]
    ppermute x6 -> x3, waiting for transfers between devices: 105 us -> 0.01 us  [send_pieces(): lax.ppermute(pieces[shift], axis, [(source, (source + shift) % count) for...]
    ppermute x6 -> x3, starting transfers between devices: 39 us -> 3.83 us  [send_pieces(): lax.ppermute(pieces[shift], axis, [(source, (source + shift) % count) for...]
    dot_general x4 -> x1, matrix products: 39.3 us -> 9.87 us  [back_project(): lax.dot_general(grad_rows, weight, (((1,), (1,)), ((), ())), preferred_el...]
    dot_general x1 -> x0, matrix products: 18.2 us -> none  [term_maker(): lax.dot_general(tokens, grad_rows, (((0,), (0,)), ((), ())), preferred_el...]
    all_gather x1, waiting for transfers between devices: 41.8 us -> 26.2 us  [per_device(): upstream_full = lax.all_gather(grad_out, 'tp', axis=1, tiled=True)]
    reduce_scatter x2 -> x0, waiting for transfers between devices: 12.8 us -> none  [the longest x1 12.8 us: per_device(): lax.psum_scatter(jnp.concatenate([flat_key, flat_value], axis=1), 'ctx',...]
    convert_element_type x5 -> x4, local copies, waits for them, and re-layouts: 12.4 us -> 4.15 us  [the longest x3 2.33 us: per_device(): part.astype(jnp.bfloat16).reshape(tok_rows, col_count)]
  transfers between devices with their start and end apart: 10 -> 5, of which waited for: 4 -> 1; matrix products, arithmetic and copies ran while one was open for 34% -> 26% of each run, Pallas kernels for 0% -> 48%
where the time goes in v1:
time: 310 us; the launch traced here: 305 us
  Pallas kernels  148 us (48%)
  matrix products  58.6 us (19%)
  local copies, waits for them, and re-layouts  29.8 us (10%)
  waiting for transfers between devices  26.9 us (9%)
  between operations  15.1 us (5%)
  other arithmetic  11.8 us (4%)
  blocking collectives  11.4 us (4%)
  starting transfers between devices  3.9 us (1%)
    pallas_call x1, Pallas kernels, tail(): pl.pallas_call(functools.partial(tail_kernel, names, cbits, tbits, per),...  148 us
    all_gather x1, waiting for transfers between devices, per_device(): upstream_full = lax.all_gather(grad_out, 'tp', axis=1, tiled=True)  26.2 us
    dot_general x3, matrix products, project(): jnp.dot(tokens, weight, preferred_element_type=jnp.float32)  21.5 us
    unnamed x70, local copies, waits for them, and re-layouts  19.4 us
    all_gather x1, blocking collectives, per_device(): lax.all_gather(jnp.concatenate([own_key, own_value], axis=1), 'ctx', axis...  11.4 us
    dot_general x12, matrix products, elementwise_product(): jnp.einsum(pattern, left_side, right_side, preferred_element_type=jnp.flo...  11.1 us
    dot_general x1, matrix products, back_project(): lax.dot_general(grad_rows, weight, (((1,), (1,)), ((), ())), preferred_el...  9.87 us
    dot_general x1, matrix products, per_device(): lax.dot_general(attn, upstream_full, (((0,), (0,)), ((), ())), preferred_...  9.2 us
  transfers between devices with their start and end apart: 5, of which 1 were waited for; matrix products, arithmetic and copies ran while one was open for 26% of the time, Pallas kernels for 48%

profile of v1, /device:TPU:0, one launch (start us, length us, event | category | flops | bytes accessed | tf_op | source)
XLA Modules:
  0.0 305.0 jit_solution(1953389921271980324)
XLA Ops:
  7.2 0.7 all-gather.2.cloned.1.call-update
  8.0 6.5 %copy.120 = bf16[512,4096]{0,1:T(8,128)(2,1)} copy(bf16[512,4096]{1,0:T(8,128)(2,1)} %param.7) | data formatting | bytes 8388608 | tf_op args[0]
  14.5 9.5 %fusion.8 = bf16[64,8,8,128]{3,1,2,0:T(8,128)(2,1)S(1)} fusion(bf16[512,4096]{1,0:T(8,128)(2,1)} %param.7, bf16[4096,1024]{1,0:T(8,128)(2,1)} %refs_8_.1), kind=kOutput, calls=%fused_computation.33 | convolution fusion | flops 4295491584 | bytes 13631488 | tf_op jit(solution)/shard_map/dot_general | solution.py:432
  24.3 7.6 %fusion.10 = bf16[64,8,8,128]{3,1,2,0:T(8,128)(2,1)S(1)} fusion(bf16[512,4096]{1,0:T(8,128)(2,1)S(1)} %copy-done.2, bf16[4096,1024]{1,0:T(8,128)(2,1)} %refs_7_.1), kind=kOutput, calls=%fused_computation.35 | convolution fusion | flops 4295491584 | bytes 13631488 | tf_op jit(solution)/shard_map/dot_general | solution.py:432
  32.2 11.4 %all_gather.7 = bf16[64,2048]{1,0:T(8,128)(2,1)S(1)} all-gather(bf16[8,2048]{1,0:T(8,128)(2,1)S(1)} %pad_maximum_fusion.2), channel_id=1, replica_groups=mesh['ctx'=8,'tp'=4] {'ctx'}, dimensions={0}, use_global_device_ids=true | all-gather | bytes 294912 | tf_op jit(solution)/shard_map/all_gather | solution.py:439
  43.6 0.8 slice_bitcast_fusion.5
  44.5 4.5 %fusion.9 = bf16[64,8,8,128]{3,1,2,0:T(8,128)(2,1)S(1)} fusion(bf16[512,4096]{1,0:T(8,128)(2,1)S(1)} %copy-done.2, bf16[4096,1024]{1,0:T(8,128)(2,1)S(1)} %bitcast.182), kind=kOutput, calls=%fused_computation.34 | convolution fusion | flops 4295491584 | bytes 13631488 | tf_op jit(solution)/shard_map/dot_general | solution.py:432
  49.8 1.2 fusion.41
  50.9 0.7 fusion.5
  51.7 0.5 fusion.6
  52.3 0.7 fusion.7
  53.6 0.8 fusion.24
  54.9 1.0 copy-done
  55.8 0.7 copy.119
  56.6 6.9 %fusion.15 = f32[512,4096]{1,0:T(8,128)S(1)} fusion(bf16[1024,4096]{1,0:T(8,128)(2,1)} %param.11, bf16[64,8,8,128]{3,2,1,0:T(8,128)(2,1)S(1)} %bitcast.173), kind=kOutput, calls=%fused_computation.45 | convolution fusion | flops 4294967296 | bytes 17825792 | tf_op jit(solution)/shard_map/dot_general | solution.py:464
  63.5 1.6 constant_dynamic-slice_fusion
  65.0 1.8 dynamic-slice_convert_fusion
  66.9 26.2 %all-gather.2.cloned.1.call-done = bf16[512,4096]{1,0:T(8,128)(2,1)} async-done(((bf16[512,1024]{1,0:T(8,128)(2,1)}), bf16[512,4096]{1,0:T(8,128)(2,1)}) %all-gather.2.cloned.1.call-update) | async-done | bytes 4194320 | tf_op jit(solution)/shard_map/all_gather | solution.py:429
  93.0 9.2 %convolution_convert_fusion = bf16[1024,4096]{1,0:T(8,128)(2,1)} fusion(bf16[512,4096]{1,0:T(8,128)(2,1)} %all-gather.2.cloned.1.call-done, bf16[64,8,8,128]{3,2,1,0:T(8,128)(2,1)S(1)} %bitcast.174), kind=kOutput, calls=%fused_computation | convolution fusion | flops 4299161600 | bytes 13631488 | tf_op jit(solution)/shard_map/dot_general | solution.py:485
  102.3 0.9 copy-done.18
  103.2 9.9 %fusion.11 = bf16[64,8,8,128]{3,1,2,0:T(8,128)(2,1)S(1)} fusion(bf16[512,4096]{1,0:T(8,128)(2,1)} %all-gather.2.cloned.1.call-done, bf16[1024,4096]{1,0:T(8,128)(2,1)} %param.11), kind=kOutput, calls=%fused_computation.36 | convolution fusion | flops 4295491584 | bytes 13631488 | tf_op jit(solution)/shard_map/dot_general | solution.py:101
  113.8 0.7 copy-done.1
  114.5 0.6 multiply_reduce_fusion
  115.2 1.1 fusion.3
  116.3 1.0 copy-done.6
  117.7 0.7 copy.248
  118.5 0.6 copy-done.11
  119.1 1.8 fusion.43
  121.0 2.6 multiply_convert_fusion
  124.7 0.5 copy-done.15
  125.2 0.7 copy.136
  125.9 1.3 copy.244
  127.2 0.7 copy.134
  127.9 1.3 copy.245
  129.2 0.5 fusion.28
  129.7 0.7 copy-done.7
  130.4 0.5 fusion.1
  131.0 0.9 copy.132
  131.9 1.2 copy.246
  133.2 1.1 collective-permute-start.1
  134.2 2.8 collective-permute-start.2
  137.0 0.6 pad_maximum_fusion.1.refs_4_
  137.6 0.8 pad_maximum_fusion.refs_5_
  138.4 147.6 %tail.1 = (f32[3,512,1024]{2,1,0:T(8,128)}, bf16[512,1024]{1,0:T(8,128)(2,1)}) custom-call(bf16[4096,512]{1,0:T(8,128)(2,1)} %bitcast.164, bf16[512,1024]{1,0:T(8,128)(2,1)} %bitcast.175, bf16[512,1024]{1,0:T(8,128)(2,1)} %bitcast.172, bf16[512,1024]{1,0:T(8,128)(2,1)} %bitcast.171, f32[2,8,1024]{2,1,0:T(8,128)} %pad_maximum_fusion.1.refs_4_, ...), custom_call_target="tpu_custom_call" | custom-call | flops 25769803776 | bytes 32505856 | tf_op jit(solution)/shard_map/tail/pallas_call | solution.py:390
  286.1 5.0 %add_convert_fusion = bf16[512,1024]{1,0:T(8,128)(2,1)} fusion(bf16[512,1024]{1,0:T(8,128)(2,1)} %collective-permute-done.2, bf16[512,1024]{1,0:T(8,128)(2,1)} %collective-permute-done.1, bf16[512,1024]{1,0:T(8,128)(2,1)} %collective-permute-done, f32[512,1024]{1,0:T(8,128)} %constant_dynamic-slice_fusion, bf16[512,4096]{1,0:T(8,128)(2,1)} %param.7, ...), kind=kLoop, calls=%fused_computation.13 | loop fusion | flops 4718592 | bytes 7340036 | tf_op jit(solution)/shard_map/convert_element_type | solution.py:514
  291.0 2.8 slice_bitcast_fusion
  293.9 2.9 convert_element_type.103
  296.8 1.0 copy.250
  (89 shorter events, 5.0 us)
Async XLA Ops:
  7.2 85.9 %all-gather.2.cloned.1.call-start = ((), (), s32[]{:S(2)}) async-start(), calls=%async_computation.1 | async-start | bytes 5242880 | tf_op jit(solution)/shard_map/all_gather | solution.py:429
  7.9 286.0 %reduce-scatter.2.cloned.1.call-start = ((), (), s32[]{:S(2)}) async-start(), calls=%async_computation.2 | async-start | bytes 9437184 | tf_op jit(solution)/shard_map/reduce_scatter | solution.py:488
  14.5 9.8 %copy-start.2 = (bf16[512,4096]{1,0:T(8,128)(2,1)S(1)}, bf16[512,4096]{1,0:T(8,128)(2,1)}, u32[]{:S(2)}) copy-start(bf16[512,4096]{1,0:T(8,128)(2,1)} %param.7) | copy-start | bytes 12582916
  24.0 20.5 %slice-start = ((s8[8388608]{0:T(1024)(128)(4,1)}), s8[4194304]{0:T(1024)(128)(4,1)S(1)}, s32[]{:S(2)}) async-start(s8[8388608]{0:T(1024)(128)(4,1)} %bitcast.181), calls=%async_computation.3 | async-start | bytes 8388608
  24.3 29.3 %copy-start.12 = (bf16[64,8,8,128]{3,2,1,0:T(8,128)(2,1)}, bf16[64,8,8,128]{3,2,1,0:T(8,128)(2,1)S(1)}, u32[]{:S(2)}) copy-start(bf16[64,8,8,128]{3,2,1,0:T(8,128)(2,1)S(1)} %copy.160) | copy-start | bytes 3145732
  24.3 20.1 %slice-start.1 = ((s8[8388608]{0:T(1024)(128)(4,1)}), s8[4194304]{0:T(1024)(128)(4,1)S(1)}, s32[]{:S(2)}) async-start(s8[8388608]{0:T(1024)(128)(4,1)} %bitcast.181), calls=%async_computation.4 | async-start | bytes 8388608
  32.2 18.8 %copy-start.4 = (bf16[64,8,8,128]{3,2,1,0:T(8,128)(2,1)}, bf16[64,8,8,128]{3,2,1,0:T(8,128)(2,1)S(1)}, u32[]{:S(2)}) copy-start(bf16[64,8,8,128]{3,2,1,0:T(8,128)(2,1)S(1)} %copy.162) | copy-start | bytes 3145732
  48.9 0.7 copy-start.25
  51.6 1.9 copy-start.10
  52.3 1.3 copy-start.19
  53.0 1.3 copy-start.23
  54.9 1.0 copy-start
  102.2 0.9 copy-start.18
  113.1 1.4 copy-start.1
  115.1 2.6 copy-start.21
  116.3 1.0 copy-start.6
  117.3 1.8 copy-start.11
  117.3 1.8 copy-start.20
  117.3 1.8 copy-start.24
  119.1 1.9 copy-start.13
  119.1 1.9 copy-start.22
  123.6 1.0 copy-start.8
  123.6 1.6 copy-start.15
  127.2 2.0 copy-start.5
  127.2 2.0 copy-start.9
  129.2 1.2 copy-start.7
  129.2 1.2 copy-start.17
  130.9 6.7 %copy-start.16 = (f32[8,8,8,128]{3,2,0,1:T(8,128)S(1)}, f32[8,8,8,128]{3,2,0,1:T(8,128)}, u32[]{:S(2)}) copy-start(f32[8,8,8,128]{3,2,0,1:T(8,128)} %copy.248) | copy-start | bytes 786436
  133.2 152.9 %collective-permute-start = (bf16[512,1024]{1,0:T(8,128)(2,1)}, bf16[512,1024]{1,0:T(8,128)(2,1)}, u32[]{:S(2)}, u32[]{:S(2)}) collective-permute-start(bf16[512,1024]{1,0:T(8,128)(2,1)} %get-tuple-element.22), channel_id=1, source_target_pairs={{0,1},{1,2},{2,3},{3,0},{4,5},{5,6},{6,7},{7,4},{8,9},{9,10},{10,1... | collective-permute-start | bytes 3145736 | tf_op jit(solution)/shard_map/ppermute | solution.py:120
  133.2 152.9 %collective-permute-start.1 = (bf16[512,1024]{1,0:T(8,128)(2,1)}, bf16[512,1024]{1,0:T(8,128)(2,1)}, u32[]{:S(2)}, u32[]{:S(2)}) collective-permute-start(bf16[512,1024]{1,0:T(8,128)(2,1)} %get-tuple-element.23), channel_id=1, source_target_pairs={{0,2},{1,3},{2,0},{3,1},{4,6},{5,7},{6,4},{7,5},{8,10},{9,11},{10,... | collective-permute-start | bytes 3145736 | tf_op jit(solution)/shard_map/ppermute | solution.py:120
  134.2 151.8 %collective-permute-start.2 = (bf16[512,1024]{1,0:T(8,128)(2,1)}, bf16[512,1024]{1,0:T(8,128)(2,1)}, u32[]{:S(2)}, u32[]{:S(2)}) collective-permute-start(bf16[512,1024]{1,0:T(8,128)(2,1)} %get-tuple-element.24), channel_id=1, source_target_pairs={{0,3},{1,0},{2,1},{3,2},{4,7},{5,4},{6,5},{7,6},{8,11},{9,8},{10,9... | collective-permute-start | bytes 3145736 | tf_op jit(solution)/shard_map/ppermute | solution.py:120
  286.1 5.0 %copy-start.3 = (f32[3,512,1024]{2,1,0:T(8,128)S(1)}, f32[3,512,1024]{2,1,0:T(8,128)}, u32[]{:S(2)}) copy-start(f32[3,512,1024]{2,1,0:T(8,128)} %get-tuple-element.29) | copy-start | bytes 18874372
  293.9 2.9 copy-start.14
Sparse Core Ops, SparseCore 0:
  9.5 83.4 all-gather.1
  102.4 87.2 reduce-scatter.1

commit v2 on v1

--- a/solution.py
+++ b/solution.py
@@ -52,55 +52,7 @@
     combined_output = elementwise_product(
         "jvyb,jbvo->jyvo", local_weight, value_row_matrix
     ) + elementwise_product("gtuv,vuk->gtuk", distant_weight, summary_value)
-    return (combined_output.astype(jnp.bfloat16), local_weight, distant_weight)
-
-
-def attend_back(
-    query_row_matrix,
-    key_row_matrix,
-    value_row_matrix,
-    summary_key,
-    summary_value,
-    combined_output,
-    local_weight,
-    distant_weight,
-    incoming_gradient,
-    score_scale_factor,
-):
-    row_delta = jnp.sum(
-        combined_output.astype(jnp.float32) * incoming_gradient.astype(jnp.float32), axis=3
-    )
-    near_d = elementwise_product("nqhd,nkhd->nhqk", incoming_gradient, value_row_matrix)
-    distant_gradient_term = elementwise_product("yzxo,lxo->yzxl", incoming_gradient, summary_value)
-    local_score_sum = (
-        local_weight.astype(jnp.float32) * (near_d - jnp.transpose(row_delta, (0, 2, 1))[..., None])
-    ).astype(jnp.bfloat16)
-    distant_score_sum = (
-        distant_weight.astype(jnp.float32) * (distant_gradient_term - row_delta[..., None])
-    ).astype(jnp.bfloat16)
-    query_gradient = (
-        elementwise_product("jvyb,jbvo->jyvo", local_score_sum, key_row_matrix)
-        + elementwise_product("gtuv,vuk->gtuk", distant_score_sum, summary_key)
-    ) * score_scale_factor
-    d_key = (
-        elementwise_product("nhqk,nqhd->nkhd", local_score_sum, query_row_matrix)
-        * score_scale_factor
-    )
-    d_value = elementwise_product("nhqk,nqhd->nkhd", local_weight, incoming_gradient)
-    summary_key_gradient = (
-        elementwise_product("agwi,agwu->iwu", distant_score_sum, query_row_matrix)
-        * score_scale_factor
-    )
-    summary_value_gradient = elementwise_product(
-        "agwi,agwu->iwu", distant_weight, incoming_gradient
-    )
-    return (query_gradient, d_key, d_value, summary_key_gradient, summary_value_gradient)
-
-
-def back_project(grad_rows, weight):
-    return lax.dot_general(
-        grad_rows, weight, (((1,), (1,)), ((), ())), preferred_element_type=jnp.float32
-    )
+    return combined_output.astype(jnp.bfloat16)
 
 
 def column_pieces(partial, axis):
@@ -122,19 +74,22 @@
     ]
 
 
-def tail_kernel(names, cbits, tbits, per, *refs):
-    turned_ref, dq_ref, dk_ref, dv_ref, edge_ref, land_ref = refs[:6]
-    wq_ref, wk_ref, wv_ref, gout_ref, out_ref, tok_ref = refs[6:12]
-    scratch = list(refs[12:])
-    grad_ref, weight_buf, total_ref, landed_ref = scratch[:4]
-    sent, landed = scratch[4 : 4 + cbits], scratch[4 + cbits : 4 + 2 * cbits]
-    scratch = scratch[4 + 2 * cbits :]
+def tail_kernel(names, scale, cbits, tbits, per, *refs):
+    up_ref, turned_ref, attn_ref, query_ref, key_ref, value_ref, wout_ref = refs[:7]
+    wq_ref, wk_ref, wv_ref, sk_ref, sv_ref, mask_ref, gout_ref, out_ref, tok_ref = refs[7:16]
+    scratch = list(refs[16:])
+    q_ref, wout_buf, edge_ref, land_ref, head_sem = scratch[:5]
+    scratch = scratch[5:]
+    left_ref, grad_ref, weight_buf, total_ref, landed_ref = scratch[:5]
+    sent, landed = scratch[5 : 5 + cbits], scratch[5 + cbits : 5 + 2 * cbits]
+    scratch = scratch[5 + 2 * cbits :]
     tsent, tlanded = scratch[:tbits], scratch[tbits : 2 * tbits]
-    load_sem, weight_sem, land_send, land_recv, send_sem, recv_sem, tsend, trecv = scratch[
+    load_sem, weight_sem, land_send, land_recv, send_sem, recv_sem, tsend, trecv, free_sem = scratch[
         2 * tbits :
     ]
     axis, other_axis = names
-    count, tiles, slots = 1 << cbits, landed[0].shape[0], sent[0].shape[0]
+    count, tiles, slots = 1 << cbits, 4 * per, sent[0].shape[0]
+    ring = landed[0].shape[0]
     rows = out_ref.shape[1]
     length, width = tok_ref.shape
     sub_width = weight_buf.shape[2]
@@ -148,9 +103,17 @@
     rest = list(range(1, cbits))
     orders = ([0] + rest, [0] + rest[::-1])
 
+    moves = (
+        (up_ref, left_ref.at[0]),
+        (attn_ref, grad_ref.at[0]),
+        (query_ref, q_ref),
+        (key_ref, grad_ref.at[2]),
+        (value_ref, grad_ref.at[3]),
+        (turned_ref, left_ref.at[1]),
+    )
     loads = [
-        pltpu.make_async_copy(ref, grad_ref.at[w], load_sem.at[w])
-        for w, ref in enumerate((dq_ref, dk_ref, dv_ref))
+        pltpu.make_async_copy(source, target, load_sem.at[w])
+        for w, (source, target) in enumerate(moves)
     ]
     for load in loads:
         load.start()
@@ -169,7 +132,7 @@
     def land_copy(shift):
         peer = (me + shift) % count
         return pltpu.make_async_remote_copy(
-            src_ref=land_ref.at[pl.ds(pl.multiple_of(peer * edge_rows, edge_rows), edge_rows), :],
+            src_ref=land_ref.at[:, pl.ds(pl.multiple_of(peer * edge_rows, edge_rows), edge_rows), :],
             dst_ref=landed_ref.at[shift - 1],
             send_sem=land_send.at[shift - 1],
             recv_sem=land_recv.at[shift - 1],
@@ -177,13 +140,13 @@
             device_id_type=MESH,
         )
 
-    for shift in range(1, count):
-        land_copy(shift).start()
+    def place(tile, stage):
+        return tile if stage else tile % ring
 
     def copy(tile, half, stage):
         return pltpu.make_async_remote_copy(
             src_ref=sent[stage].at[tile % slots, half],
-            dst_ref=landed[stage].at[tile, half],
+            dst_ref=landed[stage].at[place(tile, stage), half],
             send_sem=send_sem.at[stage, tile, half],
             recv_sem=recv_sem.at[stage, tile, half],
             device_id={axis: partner[orders[half][stage]]},
@@ -203,12 +166,46 @@
     def product(row_block, tile, half):
         which = tile // per
         start = pl.multiple_of((tile % per) * 2 * HALF + half * HALF, HALF)
-        left = turned_ref[pl.ds(pl.multiple_of(row_block * rows, rows), rows), :]
+        side = jnp.minimum(which, 1)
+        left = left_ref[side, pl.ds(pl.multiple_of(row_block * rows, rows), rows), :]
         return jnp.dot(
             left, grad_ref[which, :, pl.ds(start, HALF)], preferred_element_type=jnp.float32
         )
 
+    def first_step(tile):
+        @pl.when(tile >= slots)
+        def _():
+            for half in (0, 1):
+                copy(tile - slots, half, 0).wait_send()
+
+        which, spot = tile // per, tile % slots
+        start = pl.multiple_of((tile % per) * 2 * HALF, 2 * HALF)
+        side = jnp.minimum(which, 1)
+        for high in range(1 << (cbits - 1)):
+            row_block = (1 - digit[0]) + 2 * high
+            left = left_ref[side, pl.ds(pl.multiple_of(row_block * rows, rows), rows), :]
+            value = jnp.dot(
+                left, grad_ref[which, :, pl.ds(start, 2 * HALF)], preferred_element_type=jnp.float32
+            ).astype(jnp.bfloat16)
+            for half in (0, 1):
+                r = 0
+                for i in range(1, cbits):
+                    r += ((2 * high >> orders[half][i]) & 1) << (cbits - 1 - i)
+                sent[0][spot, half, r] = value[:, half * HALF : (half + 1) * HALF]
+        for half in (0, 1):
+            copy(tile, half, 0).start()
+
     def stage_step(tile, stage):
+        if stage == 0 and ring < tiles:
+
+            @pl.when(tile >= ring)
+            def _():
+                pl.semaphore_wait(free_sem, 1)
+
+        if stage == 0:
+            first_step(tile)
+            return
+
         for half in (0, 1):
             order = orders[half]
             if stage:
@@ -236,7 +233,7 @@
                         at += digit[order[i]] * (1 << (cbits - 1 - i))
                     if stage < cbits:
                         at += (1 - digit[order[stage]]) * (1 << (cbits - 1 - stage))
-                    value += landed[t][tile, half, at].astype(jnp.float32)
+                    value += landed[t][place(tile, t), half, at].astype(jnp.float32)
                 if stage < cbits:
                     sent[stage][tile % slots, half, r] = value.astype(jnp.bfloat16)
                 else:
@@ -244,6 +241,13 @@
                     out_ref[tile // per, :, pl.ds(start, HALF)] = value
             if stage < cbits:
                 copy(tile, half, stage).start()
+        if stage == cbits and ring < tiles:
+
+            @pl.when(tile < tiles - ring)
+            def _():
+                pl.semaphore_signal(
+                    free_sem, inc=1, device_id={axis: partner[0]}, device_id_type=MESH
+                )
 
     bases = [0]
     for stage in range(tbits):
@@ -278,21 +282,21 @@
                 for load in weight_loads(k, stage):
                     load.start()
 
-    def turn(k):
+    def turn(k, stages):
         for load in weight_loads(k, 0):
             load.wait()
         fetch(k + 1)
         value = None
         for w in range(3):
             term = lax.dot_general(
-                grad_ref[w],
+                grad_ref[1 + w],
                 weight_buf[k % 2, w],
                 (((1,), (1,)), ((), ())),
                 preferred_element_type=jnp.float32,
             )
             value = term if value is None else value + term
         total_ref[...] = value
-        for stage in range(tbits + 1):
+        for stage in stages:
 
             @pl.when((k >= bases[stage]) & (k < bases[stage + 1]))
             def _():
@@ -315,30 +319,102 @@
                     mine = gout_ref[:, pl.ds(start, sub_width)].astype(jnp.float32)
                     tok_ref[:, pl.ds(start, sub_width)] = (mine + result).astype(jnp.bfloat16)
 
+    def head_load(h):
+        start = pl.multiple_of(h * 2 * HALF, 2 * HALF)
+        return pltpu.make_async_copy(
+            wout_ref.at[pl.ds(start, 2 * HALF), :], wout_buf, head_sem.at[0]
+        )
+
+    def dot(left, right, left_dim, right_dim):
+        dims = (((left_dim,), (right_dim,)), ((), ()))
+        return lax.dot_general(left, right, dims, preferred_element_type=jnp.float32)
+
+    def attn_grads(h):
+        head_load(h).wait()
+        columns = pl.ds(pl.multiple_of(h * 2 * HALF, 2 * HALF), 2 * HALF)
+        grad_ref[1, :, columns] = dot(wout_buf[...], left_ref[0], 1, 0).T.astype(jnp.bfloat16)
+
+        @pl.when(h + 1 < per)
+        def _():
+            head_load(h + 1).start()
+
+    def attend_back(h):
+        columns = pl.ds(pl.multiple_of(h * HDIM, HDIM), HDIM)
+        sk, sv = sk_ref[:, columns], sv_ref[:, columns]
+        group = min(2 * BLOCK, length)
+        total_blocks = land_ref.shape[1]
+        spot = lax.broadcasted_iota(jnp.int32, (group, group), 0)
+        other = lax.broadcasted_iota(jnp.int32, (group, group), 1)
+        causal = (spot // BLOCK == other // BLOCK) & (other <= spot)
+        causal = jnp.where(causal, 1.0, 0.0)
+        land_key = jnp.zeros(sk.shape, jnp.float32)
+        land_value = jnp.zeros(sk.shape, jnp.float32)
+        for g in range(length // group):
+            part = slice(g * group, (g + 1) * group)
+            q, grad = q_ref[part, columns], grad_ref[1, part, columns]
+            keys = jnp.concatenate([grad_ref[2, part, columns], sk], axis=0)
+            values = jnp.concatenate([grad_ref[3, part, columns], sv], axis=0)
+            inside = jnp.concatenate([causal, mask_ref[part, :]], axis=1) > 0.0
+            score = jnp.where(inside, dot(q, keys, 1, 1) * scale, big_negative)
+            weight = jnp.exp(score - jnp.max(score, axis=1, keepdims=True))
+            weight = weight * (1.0 / jnp.sum(weight, axis=1, keepdims=True))
+            weight = weight.astype(jnp.bfloat16)
+            attn = grad_ref[0, part, columns].astype(jnp.float32)
+            delta = jnp.sum(attn * grad.astype(jnp.float32), axis=1, keepdims=True)
+            change = weight.astype(jnp.float32) * (dot(grad, values, 1, 1) - delta)
+            change = change.astype(jnp.bfloat16)
+            dq = dot(change, keys, 1, 0) * scale
+            dk = dot(change, q, 0, 0) * scale
+            dv = dot(weight, grad, 0, 0)
+            grad_ref[1, part, columns] = dq.astype(jnp.bfloat16)
+            grad_ref[2, part, columns] = dk[:group].astype(jnp.bfloat16)
+            grad_ref[3, part, columns] = dv[:group].astype(jnp.bfloat16)
+            for b in range(group // BLOCK):
+                row = slice((b + 1) * BLOCK - 1, (b + 1) * BLOCK)
+                at = g * (group // BLOCK) + b
+                edge_ref[0, at : at + 1, columns] = dk[row, :]
+                edge_ref[1, at : at + 1, columns] = dv[row, :]
+            land_key += dk[group:]
+            land_value += dv[group:]
+        land_ref[0, :, columns] = land_key[:total_blocks]
+        land_ref[1, :, columns] = land_value[:total_blocks]
+
     def finish_edges():
-        loads[1].wait()
-        loads[2].wait()
         for shift in range(1, count):
             land_copy(shift).wait_recv()
-        columns = edge_ref.shape[2]
         own = pl.ds(pl.multiple_of(me * edge_rows, edge_rows), edge_rows)
         for p in (0, 1):
-            part = slice(p * columns, (p + 1) * columns)
-            total = edge_ref[p] + land_ref[own, part]
+            total = edge_ref[p] + land_ref[p, own, :]
             for shift in range(1, count):
-                total += landed_ref[shift - 1, :, part]
+                total += landed_ref[shift - 1, p]
             for j in range(edge_rows):
                 chunk = slice((j + 1) * BLOCK - 16, (j + 1) * BLOCK)
-                old = grad_ref[1 + p, chunk, :].astype(jnp.float32)
+                old = grad_ref[2 + p, chunk, :].astype(jnp.float32)
                 last = lax.broadcasted_iota(jnp.int32, old.shape, 0) == 15
                 new = jnp.where(last, total[j : j + 1, :], old)
-                grad_ref[1 + p, chunk, :] = new.astype(jnp.bfloat16)
+                grad_ref[2 + p, chunk, :] = new.astype(jnp.bfloat16)
 
     fetch(0)
-    loads[0].wait()
+    head_load(0).start()
+    for load in loads[:5]:
+        load.wait()
+
+    def head_body(e, i):
+        attend_back(i * (2 * HALF // HDIM) + e)
+        return i
+
+    first = per
+    second = first + bases[1] // 2 + 4
     lags = [0] + [2 * s - 1 for s in range(1, cbits + 1)]
 
     def body(i, carry):
+        @pl.when(i == per)
+        def _():
+            loads[5].wait()
+
+            for shift in range(1, count):
+                land_copy(shift).start()
+
         for stage in range(cbits, -1, -1):
             tile = i - lags[stage]
 
@@ -346,17 +422,27 @@
             def _():
                 stage_step(tile, stage)
 
-        @pl.when(i == 0)
+        @pl.when(i < per)
+        def _():
+            attn_grads(i)
+            lax.fori_loop(0, 2 * HALF // HDIM, head_body, i)
+
+        @pl.when(i == per)
         def _():
             finish_edges()
 
-        @pl.when((i >= 1) & (i <= turns))
+        @pl.when((i >= first) & (i < first + bases[1] // 2))
         def _():
-            turn(i - 1)
+            turn(2 * (i - first), (0,))
+            turn(2 * (i - first) + 1, (0,))
+
+        @pl.when((i >= second) & (i < second + turns - bases[1]))
+        def _():
+            turn(bases[1] + i - second, range(1, tbits + 1))
 
         return carry
 
-    lax.fori_loop(0, max(tiles + lags[cbits], turns + 1), body, 0)
+    lax.fori_loop(0, max(tiles + lags[cbits], second + turns - bases[1]), body, 0)
     for tile in range(max(tiles - slots, 0), tiles):
         for half in (0, 1):
             for stage in range(cbits):
@@ -368,55 +454,71 @@
         land_copy(shift).wait_send()
 
 
-def tail(turned, grads, edges, land, weights, grad_out, names, call):
+def tail(upstream, turned, rows_in, weights, summaries, allowed, grad_out, names, scale, call):
     axis, other_axis = names
     count, other_count = lax.axis_size(axis), lax.axis_size(other_axis)
     cbits, tbits = count.bit_length() - 1, other_count.bit_length() - 1
     depth, length = turned.shape
-    columns = grads[0].shape[1]
+    columns = rows_in[0].shape[1]
     width = grad_out.shape[1]
     rows = depth // count
     per = columns // (2 * HALF)
-    tiles = 3 * per
-    slots = min(4, tiles)
+    tiles = 4 * per
+    slots = min(3, tiles)
+    ring = min(tiles, 2 * cbits + 2)
     sub_width = min(2 * HALF, width)
     subs = width // sub_width
     blocks = [1 << (cbits - 1 - stage) for stage in range(cbits)]
     tblocks = [subs << (tbits - 1 - stage) for stage in range(tbits)]
-    edge_rows = edges.shape[1]
+    edge_rows = length // BLOCK
+    total_blocks = summaries[0].shape[0]
+    spare = -total_blocks % HALF
+    summaries = [jnp.pad(part, ((0, spare), (0, 0))) for part in summaries]
+    mask = jnp.repeat(allowed.astype(jnp.float32), BLOCK, axis=0)
+    mask = jnp.pad(mask, ((0, 0), (0, spare)))
     vmem = pl.BlockSpec(memory_space=pltpu.VMEM)
     hbm = pl.BlockSpec(memory_space=pl.ANY)
     dma = pltpu.SemaphoreType.DMA
     return pl.pallas_call(
-        functools.partial(tail_kernel, names, cbits, tbits, per),
+        functools.partial(tail_kernel, names, scale, cbits, tbits, per),
         out_shape=[
-            jax.ShapeDtypeStruct((3, rows, columns), jnp.float32),
+            jax.ShapeDtypeStruct((4, rows, columns), jnp.float32),
             jax.ShapeDtypeStruct((length, width), jnp.bfloat16),
         ],
-        in_specs=[vmem, hbm, hbm, hbm, vmem, vmem, hbm, hbm, hbm, vmem],
+        in_specs=[hbm] * 10 + [vmem] * 4,
         out_specs=[vmem, vmem],
         scratch_shapes=[
-            pltpu.VMEM((3, length, columns), jnp.bfloat16),
+            pltpu.VMEM((length, columns), jnp.bfloat16),
+            pltpu.VMEM((2 * HALF, depth), jnp.bfloat16),
+            pltpu.VMEM((2, edge_rows, columns), jnp.float32),
+            pltpu.VMEM((2, total_blocks, columns), jnp.float32),
+            dma((1,)),
+            pltpu.VMEM((2, depth, length), jnp.bfloat16),
+            pltpu.VMEM((4, length, columns), jnp.bfloat16),
             pltpu.VMEM((2, 3, sub_width, columns), jnp.bfloat16),
             pltpu.VMEM((length, sub_width), jnp.float32),
-            pltpu.VMEM((count - 1, edge_rows, 2 * columns), jnp.float32),
+            pltpu.VMEM((count - 1, 2, edge_rows, columns), jnp.float32),
         ]
         + [pltpu.VMEM((slots, 2, n, rows, HALF), jnp.bfloat16) for n in blocks]
-        + [pltpu.VMEM((tiles, 2, n, rows, HALF), jnp.bfloat16) for n in blocks]
+        + [
+            pltpu.VMEM((tiles if stage else ring, 2, n, rows, HALF), jnp.bfloat16)
+            for stage, n in enumerate(blocks)
+        ]
         + [pltpu.VMEM((n, length, sub_width), jnp.bfloat16) for n in tblocks] * 2
-        + [dma((3,)), dma((2, 3)), dma((count - 1,)), dma((count - 1,))]
+        + [dma((6,)), dma((2, 3)), dma((count - 1,)), dma((count - 1,))]
         + [dma((cbits, tiles, 2)), dma((cbits, tiles, 2))]
-        + [dma((tbits, tblocks[0])), dma((tbits, tblocks[0]))],
+        + [dma((tbits, tblocks[0])), dma((tbits, tblocks[0]))]
+        + [pltpu.SemaphoreType.REGULAR],
         compiler_params=pltpu.CompilerParams(
             collective_id=call, has_side_effects=True, vmem_limit_bytes=63 * 1024 * 1024
         ),
         cost_estimate=pl.CostEstimate(
-            flops=12 * depth * length * columns,
+            flops=14 * depth * length * columns,
             bytes_accessed=2 * (depth * length + 3 * length * columns + 3 * depth * columns),
             transcendentals=0,
         ),
         name="tail",
-    )(turned, *grads, edges, land, *weights, grad_out)
+    )(upstream, turned, *rows_in, *weights, *summaries, mask, grad_out)
 
 
 def per_device(tokens, w_query, w_key, w_value, w_out, block_doc, grad_out):
@@ -426,23 +528,24 @@
     blocks = tok_rows // BLOCK
     head_count = col_count // HDIM
     block_shape = (blocks, BLOCK, head_count, HDIM)
-    upstream_full = lax.all_gather(grad_out, "tp", axis=1, tiled=True)
+    upstream = lax.all_gather(grad_out.T, "tp", axis=0, tiled=True)
 
     def project(weight):
         return jnp.dot(tokens, weight, preferred_element_type=jnp.float32).astype(jnp.bfloat16)
 
-    query_row_matrix = project(w_query).reshape(block_shape)
-    key_row_matrix = project(w_key).reshape(block_shape)
-    value_row_matrix = project(w_value).reshape(block_shape)
+    query, key, value = project(w_query), project(w_key), project(w_value)
+    query_row_matrix = query.reshape(block_shape)
+    key_row_matrix = key.reshape(block_shape)
+    value_row_matrix = value.reshape(block_shape)
     own_key = key_row_matrix[:, BLOCK - 1].reshape(blocks, col_count)
     own_value = value_row_matrix[:, BLOCK - 1].reshape(blocks, col_count)
     summary = lax.all_gather(
         jnp.concatenate([own_key, own_value], axis=1), "ctx", axis=0, tiled=True
     )
-    summary_key, summary_value = summary[:, :col_count], summary[:, col_count:]
-    total_blocks = summary_key.shape[0]
-    summary_key = summary_key.reshape(total_blocks, head_count, HDIM)
-    summary_value = summary_value.reshape(total_blocks, head_count, HDIM)
+    flat_key, flat_value = summary[:, :col_count], summary[:, col_count:]
+    total_blocks = summary.shape[0]
+    summary_key = flat_key.reshape(total_blocks, head_count, HDIM)
+    summary_value = flat_value.reshape(total_blocks, head_count, HDIM)
     first_block = lax.axis_index("ctx") * blocks
     query_ids = first_block + jnp.arange(blocks, dtype=jnp.int32)
     own_doc = lax.dynamic_slice_in_dim(block_doc, first_block, blocks, 0)
@@ -450,7 +553,7 @@
     allowed = (block_ids[None, :] < query_ids[:, None]) & (block_doc[None, :] == own_doc[:, None])
     positions = jnp.arange(BLOCK, dtype=jnp.int32)
     causal = positions[None, :] <= positions[:, None]
-    combined_output, local_weight, distant_weight = attend(
+    combined_output = attend(
         query_row_matrix,
         key_row_matrix,
         value_row_matrix,
@@ -464,45 +567,18 @@
     partial_value = jnp.dot(attn, w_out, preferred_element_type=jnp.float32)
     turned = tokens.T
     pieces = column_pieces(partial_value, "tp")
-    upstream_full, pieces, turned = lax.optimization_barrier((upstream_full, pieces, turned))
+    upstream, pieces, turned = lax.optimization_barrier((upstream, pieces, turned))
     moved = send_pieces(pieces, "tp")
-    d_attn = back_project(upstream_full, w_out).astype(jnp.bfloat16)
-    grads = attend_back(
-        query_row_matrix,
-        key_row_matrix,
-        value_row_matrix,
-        summary_key,
-        summary_value,
-        combined_output,
-        local_weight,
-        distant_weight,
-        d_attn.reshape(block_shape),
-        score_scale_factor,
-    )
-    query_gradient, d_key, d_value, summary_key_gradient, summary_value_gradient = grads
-    flat_key = summary_key_gradient.reshape(total_blocks, col_count)
-    flat_value = summary_value_gradient.reshape(total_blocks, col_count)
-    out_term = lax.dot_general(
-        attn, upstream_full, (((0,), (0,)), ((), ())), preferred_element_type=jnp.float32
-    )
-    grad_out_weight = lax.psum_scatter(
-        out_term.astype(jnp.bfloat16), "ctx", scatter_dimension=1, tiled=True
-    ).astype(jnp.float32)
-    edges = jnp.stack(
-        [d_key[:, BLOCK - 1].reshape(blocks, col_count), d_value[:, BLOCK - 1].reshape(blocks, col_count)]
-    )
-    rows_of = [
-        part.astype(jnp.bfloat16).reshape(tok_rows, col_count)
-        for part in (query_gradient, d_key, d_value)
-    ]
     joined, grad_tokens = tail(
+        upstream,
         turned,
-        rows_of,
-        edges,
-        jnp.concatenate([flat_key, flat_value], axis=1),
-        (w_query, w_key, w_value),
+        (attn, query, key, value),
+        (w_out, w_query, w_key, w_value),
+        (flat_key, flat_value),
+        allowed,
         grad_out,
         ("ctx", "tp"),
+        score_scale_factor,
         0,
     )
     joined, moved = lax.optimization_barrier((joined, moved))
@@ -512,7 +588,7 @@
     for piece in moved:
         summed = summed + piece.astype(jnp.float32)
     output = summed.astype(jnp.bfloat16)
-    return (output, grad_tokens, joined[0], joined[1], joined[2], grad_out_weight)
+    return (output, grad_tokens, joined[1], joined[2], joined[3], joined[0].T)
 
 
 def solution(mesh):

time: 310 us -> 283 us (0.913); the launches traced: 305 us -> 283 us
  matrix products: 58.6 us -> 31.9 us
  Pallas kernels: 148 us -> 163 us
  other arithmetic: 11.8 us -> 5.55 us
  waiting for transfers between devices: 26.9 us -> 22.8 us
    dot_general x2 -> x0, matrix products: 19.1 us -> none  [the longest x1 9.87 us: back_project(): lax.dot_general(grad_rows, weight, (((1,), (1,)), ((), ())), preferred_el...]
    pallas_call x1, Pallas kernels: 148 us -> 163 us  [tail(): pl.pallas_call(functools.partial(tail_kernel, names, scale, cbits, tbits,...]
    dot_general x12 -> x4, matrix products: 11.1 us -> 3.29 us  [elementwise_product(): jnp.einsum(pattern, left_side, right_side, preferred_element_type=jnp.flo...]
    transpose x0 -> x1, local copies, waits for them, and re-layouts: none -> 7.48 us  [per_device(): return (output, grad_tokens, joined[1], joined[2], joined[3], joined[0].T)]
    all_gather x1, waiting for transfers between devices: 26.2 us -> 22.8 us  [per_device(): upstream = lax.all_gather(grad_out.T, 'tp', axis=0, tiled=True)]
    convert_element_type x2 -> x1, other arithmetic: 3.43 us -> 0.08 us  [tail(): mask = jnp.repeat(allowed.astype(jnp.float32), BLOCK, axis=0)]
    unnamed x70 -> x27, local copies, waits for them, and re-layouts: 19.4 us -> 16.2 us
  transfers between devices with their start and end apart: 5 -> 4, of which waited for: 1 -> 1; matrix products, arithmetic and copies ran while one was open for 26% -> 17% of each run, Pallas kernels for 48% -> 58%
where the time goes in v2:
time: 283 us
  Pallas kernels  163 us (58%)
  matrix products  31.9 us (11%)
  local copies, waits for them, and re-layouts  30.2 us (11%)
  waiting for transfers between devices  22.8 us (8%)
  between operations  14.4 us (5%)
  blocking collectives  11.3 us (4%)
  other arithmetic  5.55 us (2%)
  starting transfers between devices  3.87 us (1%)
    pallas_call x1, Pallas kernels, tail(): pl.pallas_call(functools.partial(tail_kernel, names, scale, cbits, tbits,...  163 us
    all_gather x1, waiting for transfers between devices, per_device(): upstream = lax.all_gather(grad_out.T, 'tp', axis=0, tiled=True)  22.8 us
    dot_general x3, matrix products, project(): jnp.dot(tokens, weight, preferred_element_type=jnp.float32)  21.7 us
    unnamed x27, local copies, waits for them, and re-layouts  16.2 us
    all_gather x1, blocking collectives, per_device(): lax.all_gather(jnp.concatenate([own_key, own_value], axis=1), 'ctx', axis...  11.3 us
    transpose x1, local copies, waits for them, and re-layouts, per_device(): return (output, grad_tokens, joined[1], joined[2], joined[3], joined[0].T)  7.48 us
    dot_general x1, matrix products, per_device(): partial_value = jnp.dot(attn, w_out, preferred_element_type=jnp.float32)  6.94 us
  transfers between devices with their start and end apart: 4, of which 1 were waited for; matrix products, arithmetic and copies ran while one was open for 17% of the time, Pallas kernels for 58%

profile of v2, /device:TPU:0, one launch (start us, length us, event | category | flops | bytes accessed | tf_op | source)
XLA Modules:
  0.0 282.7 jit_solution(16647223665768048567)
XLA Ops:
  7.2 0.0 all-gather.2.cloned.1.call-start
  7.2 2.3 copy.47
  9.5 0.0 all-gather.2.cloned.1.call-update
  9.6 6.5 %copy.65 = bf16[512,4096]{0,1:T(8,128)(2,1)} copy(bf16[512,4096]{1,0:T(8,128)(2,1)} %param.7) | data formatting | bytes 8388608 | tf_op args[0]
  16.0 9.8 %fusion.27.refs_4_ = bf16[512,1024]{1,0:T(8,128)(2,1)S(1)} fusion(bf16[512,4096]{1,0:T(8,128)(2,1)} %param.7, bf16[4096,1024]{1,0:T(8,128)(2,1)} %refs_8_.1), kind=kOutput, calls=%fused_computation.59 | convolution fusion | flops 4294967296 | bytes 13631488 | tf_op jit(solution)/shard_map/dot_general | solution.py:534
  25.9 0.0 slice-start.1
  25.9 7.4 %fusion.25.refs_5_ = bf16[512,1024]{1,0:T(8,128)(2,1)S(1)} fusion(bf16[512,4096]{1,0:T(8,128)(2,1)S(1)} %copy-done.1, bf16[4096,1024]{1,0:T(8,128)(2,1)} %refs_9_.1), kind=kOutput, calls=%fused_computation.57 | convolution fusion | flops 4294967296 | bytes 13631488 | tf_op jit(solution)/shard_map/dot_general | solution.py:534
  33.3 0.3 copy.76
  33.6 0.3 copy.78
  33.9 0.4 copy-done.3
  34.4 11.3 %all_gather.7 = bf16[64,2048]{1,0:T(8,128)(2,1)S(1)} all-gather(bf16[8,2048]{1,0:T(8,128)(2,1)S(1)} %pad_maximum_fusion), channel_id=1, replica_groups=mesh['ctx'=8,'tp'=4] {'ctx'}, dimensions={0}, use_global_device_ids=true | all-gather | bytes 294912 | tf_op jit(solution)/shard_map/all_gather | solution.py:542
  45.6 0.1 fusion.23
  45.7 0.7 pad.12.refs_11_
  46.4 0.7 pad.11.refs_10_
  47.2 0.0 slice-done
  47.2 0.0 slice-done.1
  47.2 4.5 %fusion.26.refs_3_ = bf16[512,1024]{1,0:T(8,128)(2,1)S(1)} fusion(bf16[512,4096]{1,0:T(8,128)(2,1)S(1)} %copy-done.1, bf16[4096,1024]{1,0:T(8,128)(2,1)S(1)} %bitcast.91), kind=kOutput, calls=%fused_computation.58 | convolution fusion | flops 4294967296 | bytes 13631488 | tf_op jit(solution)/shard_map/dot_general | solution.py:534
  51.7 0.0 copy-start.4
  51.7 0.0 copy-start.6
  51.7 0.9 copy-done.4
  52.7 0.3 copy.77
  53.0 0.1 dynamic_slice.19
  53.1 0.1 fusion.21
  53.1 1.2 fusion.24
  54.3 0.7 fusion.1
  55.0 0.5 fusion.2
  55.6 0.7 fusion.3
  56.3 0.8 fusion.5
  57.1 0.7 fusion
  57.7 0.7 copy.64
  58.4 1.2 copy.113
  59.7 0.7 pad.13.refs_12_
  60.5 6.9 %fusion.20 = f32[512,4096]{1,0:T(8,128)S(1)} fusion(bf16[1024,4096]{1,0:T(8,128)(2,1)} %refs_6_.1, bf16[64,8,8,128]{3,2,1,0:T(8,128)(2,1)S(1)} %bitcast.77), kind=kOutput, calls=%fused_computation.53 | convolution fusion | flops 4294967296 | bytes 17825792 | tf_op jit(solution)/shard_map/dot_general | solution.py:567
  67.4 1.6 constant_dynamic-slice_fusion
  69.0 1.8 dynamic-slice_convert_fusion
  70.8 22.8 %all-gather.2.cloned.1.call-done.refs_0_ = bf16[4096,512]{1,0:T(8,128)(2,1)} async-done(((bf16[1024,512]{1,0:T(8,128)(2,1)}), bf16[4096,512]{1,0:T(8,128)(2,1)}) %all-gather.2.cloned.1.call-update) | async-done | bytes 4194320 | tf_op jit(solution)/shard_map/all_gather | solution.py:531
  93.6 0.0 collective-permute-start
  93.6 1.1 collective-permute-start.1
  94.8 2.7 collective-permute-start.2
  97.4 162.7 %tail.1 = (f32[4,512,1024]{2,1,0:T(8,128)}, bf16[512,1024]{1,0:T(8,128)(2,1)}) custom-call(bf16[4096,512]{1,0:T(8,128)(2,1)} %all-gather.2.cloned.1.call-done.refs_0_, bf16[4096,512]{1,0:T(8,128)(2,1)} %bitcast.74, bf16[512,1024]{1,0:T(8,128)(2,1)} %bitcast.88, bf16[512,1024]{1,0:T(8,128)(2,1)} %copy-done.4, bf16[512,1024]{1,0:T(8,128)(2,1)} %copy-done.2, ...), custom_call_target="tpu_custom_call" | custom-call | flops 30064771072 | bytes 32505856 | tf_op jit(solution)/shard_map/tail/pallas_call | solution.py:482
  260.1 0.0 collective-permute-done
  260.1 0.0 collective-permute-done.1
  260.2 0.0 collective-permute-done.2
  260.2 7.5 %slice_bitcast_fusion = (f32[1024,512]{0,1:T(8,128)}, f32[512,1024]{1,0:T(8,128)}, f32[512,1024]{1,0:T(8,128)}, f32[512,1024]{1,0:T(8,128)}) fusion(f32[4,512,1024]{2,1,0:T(8,128)} %get-tuple-element.29), kind=kLoop, calls=%fused_computation.6 | loop fusion | bytes 16777216 | tf_op jit(solution)/shard_map/transpose | solution.py:591
  267.7 3.0 %copy.66 = f32[1024,512]{1,0:T(8,128)} copy(f32[1024,512]{0,1:T(8,128)} %get-tuple-element.50) | data formatting | bytes 4194304
  270.7 4.2 %add_convert_fusion = bf16[512,1024]{1,0:T(8,128)(2,1)} fusion(bf16[512,1024]{1,0:T(8,128)(2,1)} %collective-permute-done.2, bf16[512,1024]{1,0:T(8,128)(2,1)} %collective-permute-done.1, bf16[512,1024]{1,0:T(8,128)(2,1)} %collective-permute-done, f32[512,1024]{1,0:T(8,128)S(1)} %copy-done, bf16[512,4096]{1,0:T(8,128)(2,1)} %param.7, s32[]{:T(128)S(6)} %select_n.45), kind=kLoop, calls=%fused_computation.10 | loop fusion | flops 4718592 | bytes 7340036 | tf_op jit(solution)/shard_map/convert_element_type | solution.py:590
  274.9 0.0 copy-done.5
  274.9 1.0 copy.115
  (25 shorter events, 0.2 us)
Async XLA Ops:
  7.2 86.4 %all-gather.2.cloned.1.call-start = ((), (), s32[]{:S(2)}) async-start(), calls=%async_computation | async-start | bytes 5242880 | tf_op jit(solution)/shard_map/all_gather | solution.py:531
  16.0 9.8 %copy-start.1 = (bf16[512,4096]{1,0:T(8,128)(2,1)S(1)}, bf16[512,4096]{1,0:T(8,128)(2,1)}, u32[]{:S(2)}) copy-start(bf16[512,4096]{1,0:T(8,128)(2,1)} %param.7) | copy-start | bytes 12582916
  16.0 31.1 %slice-start = ((s8[8388608]{0:T(1024)(128)(4,1)}), s8[4194304]{0:T(1024)(128)(4,1)S(1)}, s32[]{:S(2)}) async-start(s8[8388608]{0:T(1024)(128)(4,1)} %bitcast.90), calls=%async_computation.1 | async-start | bytes 8388608
  25.9 7.8 %copy-start.2 = (bf16[512,1024]{1,0:T(8,128)(2,1)}, bf16[512,1024]{1,0:T(8,128)(2,1)S(1)}, u32[]{:S(2)}) copy-start(bf16[512,1024]{1,0:T(8,128)(2,1)S(1)} %fusion.27.refs_4_) | copy-start | bytes 3145732
  25.9 21.3 %slice-start.1 = ((s8[8388608]{0:T(1024)(128)(4,1)}), s8[4194304]{0:T(1024)(128)(4,1)S(1)}, s32[]{:S(2)}) async-start(s8[8388608]{0:T(1024)(128)(4,1)} %bitcast.90), calls=%async_computation.2 | async-start | bytes 8388608
  33.3 1.0 copy-start.3
  51.7 1.0 copy-start.4
  51.7 1.2 copy-start.6
  93.6 166.5 %collective-permute-start = (bf16[512,1024]{1,0:T(8,128)(2,1)}, bf16[512,1024]{1,0:T(8,128)(2,1)}, u32[]{:S(2)}, u32[]{:S(2)}) collective-permute-start(bf16[512,1024]{1,0:T(8,128)(2,1)} %get-tuple-element.22), channel_id=1, source_target_pairs={{0,1},{1,2},{2,3},{3,0},{4,5},{5,6},{6,7},{7,4},{8,9},{9,10},{10,1... | collective-permute-start | bytes 3145736 | tf_op jit(solution)/shard_map/ppermute | solution.py:72
  93.6 166.5 %collective-permute-start.1 = (bf16[512,1024]{1,0:T(8,128)(2,1)}, bf16[512,1024]{1,0:T(8,128)(2,1)}, u32[]{:S(2)}, u32[]{:S(2)}) collective-permute-start(bf16[512,1024]{1,0:T(8,128)(2,1)} %get-tuple-element.23), channel_id=1, source_target_pairs={{0,2},{1,3},{2,0},{3,1},{4,6},{5,7},{6,4},{7,5},{8,10},{9,11},{10,... | collective-permute-start | bytes 3145736 | tf_op jit(solution)/shard_map/ppermute | solution.py:72
  94.8 165.4 %collective-permute-start.2 = (bf16[512,1024]{1,0:T(8,128)(2,1)}, bf16[512,1024]{1,0:T(8,128)(2,1)}, u32[]{:S(2)}, u32[]{:S(2)}) collective-permute-start(bf16[512,1024]{1,0:T(8,128)(2,1)} %get-tuple-element.24), channel_id=1, source_target_pairs={{0,3},{1,0},{2,1},{3,2},{4,7},{5,4},{6,5},{7,6},{8,11},{9,8},{10,9... | collective-permute-start | bytes 3145736 | tf_op jit(solution)/shard_map/ppermute | solution.py:72
  267.7 3.0 %copy-start = (f32[512,1024]{1,0:T(8,128)S(1)}, f32[512,1024]{1,0:T(8,128)}, u32[]{:S(2)}) copy-start(f32[512,1024]{1,0:T(8,128)} %constant_dynamic-slice_fusion) | copy-start | bytes 6291460
  270.7 4.2 %copy-start.5 = (bf16[512,1024]{1,0:T(8,128)(2,1)S(1)}, bf16[512,1024]{1,0:T(8,128)(2,1)}, u32[]{:S(2)}) copy-start(bf16[512,1024]{1,0:T(8,128)(2,1)} %get-tuple-element.74) | copy-start | bytes 3145732
Sparse Core Ops, SparseCore 0:
  10.1 83.4 all-gather.1
